TPU v7x, 32 devices: a whole 2x2x4 slice. The times are simulated.
32 devices in a mesh: expert: 8 (over z, x), shard: 4 (over y, core).
Axes of the slice: x: 2, y: 2, z: 4, core: 2. Of those that a mesh axis runs over, the one named last changes fastest.
Arguments:
- tokens: bfloat16 [64, 384, 768], P(('expert', 'shard')), may hold values from -6 to 6
- cotangent: bfloat16 [64, 384, 768], P(('expert', 'shard')), may hold values from -6 to 6
- lengths: int32 [64], replicated, may hold values from 1 to 384, 18432 in all
- dealing: int32 [64], P(('expert', 'shard')), may hold values from 0 to 63, each once
- routes: int32 [64, 384, 2], P(('expert', 'shard')), may hold values from 0 to 7, all different within a row; in each aligned block of 384 rows (0 to 383, 384 to 767, ..., all dimensions but the last counted through in order) at most 192 rows name the same one
- query_weight: bfloat16 [768, 768], P('shard'), may hold values from -0.21875 to 0.21875
- key_weight: bfloat16 [768, 768], P('shard'), may hold values from -0.21875 to 0.21875
- value_weight: bfloat16 [768, 768], P('shard'), may hold values from -0.21875 to 0.21875
- output_weight: bfloat16 [768, 768], P('shard'), may hold values from -0.875 to 0.875
- router_weight: bfloat16 [768, 8], P('shard'), may hold values from -0.3125 to 0.3125
- first_gain: bfloat16 [768], P('shard'), may hold values from 0.5 to 1.5
- second_gain: bfloat16 [768], P('shard'), may hold values from 0.5 to 1.5
- position_bias: bfloat16 [12, 32], P('shard'), may hold values from -3 to 3
- inner_weight: bfloat16 [8, 768, 3072], P('expert', None, 'shard'), may hold values from -0.21875 to 0.21875
- outer_weight: bfloat16 [8, 3072, 768], P('expert', 'shard'), may hold values from -0.109375 to 0.109375
Outputs:
- result: bfloat16 [64, 384, 768], P(('expert', 'shard'))
- input_gradient: bfloat16 [64, 384, 768], P(('expert', 'shard'))
- query_gradient: float32 [768, 768], P('shard')
- key_gradient: float32 [768, 768], P('shard')
- value_gradient: float32 [768, 768], P('shard')
- output_gradient: float32 [768, 768], P('shard')
- router_gradient: float32 [768, 8], P('shard')
- first_gain_gradient: float32 [768], P('shard')
- second_gain_gradient: float32 [768], P('shard')
- bias_gradient: float32 [12, 32], P('shard')
- inner_gradient: float32 [8, 768, 3072], P('expert', None, 'shard')
- outer_gradient: float32 [8, 3072, 768], P('expert', 'shard')
Inputs may be any that keep to these rules, and one draw needn't show every extreme that they name: The lengths of all sequences; some sequence fills all 384 slots. `dealing`: each sequence number appears once. `routes`: A token's two experts differ; within one sequence no expert is chosen by more than 192 tokens, and in every draw some expert is chosen by exactly 192 tokens of some sequence.
All inputs are finite; a program needn't handle non-finite values.
Results may differ from a plain program's by a relative error of at most 0.017.
Values may be sent and summed in bfloat16 or wider, within the bound.
A program may use at most 256 MiB of HBM per device.

v0:
```python
import functools
import math

import jax
import jax.numpy as jnp
import numpy as np
from jax import lax
from jax.experimental import pallas as pl
from jax.experimental.pallas import tpu as pltpu
from jax.sharding import PartitionSpec as P

EPSILON = 1e-06
HIGH = lax.Precision.HIGHEST
NEGATIVE = -1000000000.0
INV_ROOT_TWO = 1.0 / math.sqrt(2.0)
INV_ROOT_TAU = 1.0 / math.sqrt(2.0 * math.pi)
LANES = 128


def bucket_table(length):
    distance = np.arange(length)
    scaled = 16 + np.floor(np.log(np.maximum(distance, 1) / 16.0) / np.log(8.0) * 16.0)
    return np.where(distance < 16, distance, np.minimum(scaled, 31)).astype(np.int32)


def gelu_parts(pre_act):
    normal_cdf = 0.5 * (1.0 + lax.erf(pre_act * INV_ROOT_TWO))
    return (
        pre_act * normal_cdf,
        normal_cdf + pre_act * jnp.exp(-0.5 * pre_act * pre_act) * INV_ROOT_TAU,
    )


def distance_table(length):
    offsets = np.arange(length // LANES)[:, None] * LANES
    return offsets, np.arange(2 * LANES)[None, :]


def spread_hot(length, bucket_count):
    offsets, lanes = distance_table(length)
    signed = np.where(lanes < LANES, lanes, lanes - 2 * LANES)
    distance = np.clip(offsets - signed, 0, length - 1).reshape(-1)
    return (bucket_table(length)[distance][None, :] == np.arange(bucket_count)[:, None]).astype(
        np.float32
    )


def collect_hot(length, bucket_count):
    offsets, lanes = distance_table(length)
    distance = (offsets + LANES - 1 - lanes).reshape(-1)
    inside = (distance >= 0) & (distance < length)
    table = bucket_table(length)[np.clip(distance, 0, length - 1)]
    return ((table[:, None] == np.arange(bucket_count)[None, :]) & inside[:, None]).astype(
        np.float32
    )


def half_mask(head):
    lane = lax.broadcasted_iota(jnp.int32, (1, LANES), 1)
    return (lane < LANES // 2) if head == 0 else (lane >= LANES // 2)


def only(value, head):
    return jnp.where(half_mask(head), value, jnp.zeros_like(value))


def nt_dot(left, right):
    return lax.dot_general(
        left, right, (((1,), (1,)), ((), ())), preferred_element_type=jnp.float32
    )


def tn_dot(left, right):
    return lax.dot_general(
        left, right, (((0,), (0,)), ((), ())), preferred_element_type=jnp.float32
    )


def toeplitz_block(row):
    spread = pltpu.roll(
        jnp.broadcast_to(row, (LANES, 2 * LANES)), 0, 1, stride=1, stride_axis=0
    )
    return spread[:, :LANES]


def fill_bias(bias_ref, table_ref, blocks):
    for head in range(2):
        for offset in range(blocks):
            table_ref[head, offset] = toeplitz_block(bias_ref[0, head, offset, :][None, :])


def masked_logits(query, keys, table_ref, head, block, length):
    width = (block + 1) * LANES
    bias = jnp.concatenate([table_ref[head, block - j] for j in range(block + 1)], 1)
    logits = nt_dot(query, keys) * ((LANES // 2) ** (-0.5)) + bias
    row = lax.broadcasted_iota(jnp.int32, (LANES, width), 0) + block * LANES
    column = lax.broadcasted_iota(jnp.int32, (LANES, width), 1)
    return jnp.where((column <= row) & (column < length), logits, NEGATIVE)


SLOTS = 192


def unit(value):
    return lax.rsqrt(jnp.mean(value * value, -1, keepdims=True) + EPSILON)


def column_iota(rows, columns):
    return lax.broadcasted_iota(jnp.int32, (rows, columns), 1)


def row_iota(rows, columns):
    return lax.broadcasted_iota(jnp.int32, (rows, columns), 0)


def row_places(routes_t_ref, experts, capacity):
    tokens = routes_t_ref.shape[1]
    padded = -(-experts // 16) * 16
    expert = row_iota(padded, tokens)
    hot = [expert == routes_t_ref[pick : pick + 1, :] for pick in range(2)]
    both = jnp.where(hot[0] | hot[1], 1.0, 0.0).astype(jnp.bfloat16)
    before = (row_iota(tokens, tokens) < column_iota(tokens, tokens)).astype(jnp.float32)
    rank = jnp.dot(both, before.astype(jnp.bfloat16), preferred_element_type=jnp.float32)
    slot = rank + (expert * capacity).astype(jnp.float32)
    return [jnp.sum(jnp.where(chosen, slot, 0.0), 0, keepdims=True) for chosen in hot]


def column_places(routes_ref, experts, capacity):
    tokens = routes_ref.shape[0]
    expert = column_iota(tokens, LANES)
    hot = [expert == routes_ref[:, pick : pick + 1] for pick in range(2)]
    both = jnp.where(hot[0] | hot[1], 1.0, 0.0).astype(jnp.bfloat16)
    before = (column_iota(tokens, tokens) < row_iota(tokens, tokens)).astype(jnp.float32)
    rank = jnp.dot(before.astype(jnp.bfloat16), both, preferred_element_type=jnp.float32)
    slot = rank + (expert * capacity).astype(jnp.float32)
    return [jnp.sum(jnp.where(chosen, slot, 0.0), 1, keepdims=True) for chosen in hot], hot


def one_hot(condition):
    return jnp.where(condition, 1.0, 0.0).astype(jnp.bfloat16)


def forward_math(
    experts,
    capacity,
    length,
    x_ref,
    g_ref,
    routes_ref,
    routes_t_ref,
    query_ref,
    key_ref,
    value_ref,
    output_ref,
    router_ref,
    gain_ref,
    bias_ref,
    sent_ref,
    normed_ref,
    q_ref,
    k_ref,
    v_ref,
    mix_ref,
    residual_ref,
    gates_ref,
    table_ref,
):
    tokens, width = x_ref.shape
    blocks = tokens // LANES
    inputs = x_ref[...].astype(jnp.float32)
    normed = (inputs * unit(inputs) * gain_ref[0:1, :]).astype(jnp.bfloat16)
    normed_ref[...] = normed
    for weight, out in ((query_ref, q_ref), (key_ref, k_ref), (value_ref, v_ref)):
        out[...] = jnp.dot(normed, weight[...], preferred_element_type=jnp.float32).astype(
            jnp.bfloat16
        )

    def attend(pair, carry):
        lanes = pl.ds(pl.multiple_of(pair * LANES, LANES), LANES)
        fill_bias(bias_ref.at[pl.ds(pair, 1)], table_ref, blocks)
        for block in range(blocks):
            rows = pl.ds(block * LANES, LANES)
            reach = (block + 1) * LANES
            mixed = jnp.zeros((LANES, LANES), jnp.float32)
            for head in range(2):
                logits = masked_logits(
                    only(q_ref[rows, lanes], head),
                    k_ref[:reach, lanes],
                    table_ref,
                    head,
                    block,
                    length,
                )
                exponent = jnp.exp(logits - jnp.max(logits, 1, keepdims=True))
                soft = exponent / jnp.sum(exponent, 1, keepdims=True)
                mixed = mixed + jnp.dot(
                    soft.astype(jnp.bfloat16),
                    only(v_ref[:reach, lanes], head),
                    preferred_element_type=jnp.float32,
                )
            mix_ref[rows, lanes] = mixed.astype(jnp.bfloat16)
        return carry

    lax.fori_loop(0, width // LANES, attend, 0)
    residual = inputs + jnp.dot(
        mix_ref[...], output_ref[...], preferred_element_type=jnp.float32
    )
    residual_ref[...] = residual
    normed = (residual * unit(residual) * gain_ref[1:2, :]).astype(jnp.bfloat16)
    router = jnp.dot(normed, router_ref[...], preferred_element_type=jnp.float32)
    lane = column_iota(tokens, LANES)
    chosen = [
        jnp.sum(jnp.where(lane == routes_ref[:, pick : pick + 1], router, 0.0), 1, keepdims=True)
        for pick in range(2)
    ]
    top = jnp.maximum(chosen[0], chosen[1])
    gates = [jnp.exp(value - top) for value in chosen]
    total = gates[0] + gates[1]
    gates = [value / total for value in gates]
    gates_ref[...] = jnp.where(lane == 0, gates[0], jnp.where(lane == 1, gates[1], 0.0))
    grads = [(g_ref[...].astype(jnp.float32) * gate).astype(jnp.bfloat16) for gate in gates]
    places = row_places(routes_t_ref, experts, capacity)
    slots = sent_ref.shape[2]
    for index in range(sent_ref.shape[0]):
        slot = (row_iota(slots, tokens) + index * slots).astype(jnp.float32)
        hot = [jnp.where(slot == place, 1.0, 0.0) for place in places]
        sent_ref[index, 0] = jnp.dot(
            (hot[0] + hot[1]).astype(jnp.bfloat16), normed, preferred_element_type=jnp.float32
        ).astype(jnp.bfloat16)
        sent_ref[index, 1] = (
            jnp.dot(hot[0].astype(jnp.bfloat16), grads[0], preferred_element_type=jnp.float32)
            + jnp.dot(hot[1].astype(jnp.bfloat16), grads[1], preferred_element_type=jnp.float32)
        ).astype(jnp.bfloat16)


def forward_kernel(experts, capacity, length_ref, *refs):
    forward_math(experts, capacity, length_ref[0], *refs)


def split(value):
    high = value.astype(jnp.bfloat16)
    return high, (value - high.astype(jnp.float32)).astype(jnp.bfloat16)


def norm_back(value, gain, grad):
    scale = unit(value)
    rows = value * scale
    grad_unit = grad * gain
    grad_gain = jnp.sum(grad * rows, 0, keepdims=True)
    mean = jnp.mean(grad_unit * rows, -1, keepdims=True)
    return scale * (grad_unit - rows * mean), grad_gain


def backward_math(
    experts,
    capacity,
    tick,
    length,
    x_ref,
    g_ref,
    routes_ref,
    query_ref,
    key_ref,
    value_ref,
    output_ref,
    router_ref,
    gain_ref,
    bias_ref,
    q_ref,
    k_ref,
    v_ref,
    residual_ref,
    gates_ref,
    out_rows_ref,
    back_rows_ref,
    result_ref,
    input_grad_ref,
    branch_ref,
    dq_ref,
    dk_ref,
    dv_ref,
    router_grad_ref,
    gain_grad_ref,
    diag_ref,
    grad_mix_ref,
    grad_residual_ref,
    table_ref,
    dk_sum,
    dv_sum,
    skew_ref,
):
    tokens, width = x_ref.shape
    blocks = tokens // LANES
    scale = (LANES // 2) ** (-0.5)
    grad_result = g_ref[...].astype(jnp.float32)
    residual = residual_ref[...]
    places, picks = column_places(routes_ref, experts, capacity)
    gates = [gates_ref[:, pick : pick + 1] for pick in range(2)]
    slots = out_rows_ref.shape[1]
    picked = [jnp.zeros((tokens, width), jnp.float32) for _ in range(2)]
    grad_normed = jnp.zeros((tokens, width), jnp.float32)
    for index in range(0, out_rows_ref.shape[0], 2):
        slot = (column_iota(tokens, 2 * slots) + index * slots).astype(jnp.float32)
        hot = [jnp.where(slot == place, 1.0, 0.0) for place in places]
        out_rows = out_rows_ref[index : index + 2].reshape(2 * slots, width)
        back_rows = back_rows_ref[index : index + 2].reshape(2 * slots, width)
        for pick in range(2):
            picked[pick] = picked[pick] + jnp.dot(
                hot[pick].astype(jnp.bfloat16), out_rows, preferred_element_type=jnp.float32
            )
        grad_normed = grad_normed + jnp.dot(
            (hot[0] + hot[1]).astype(jnp.bfloat16), back_rows, preferred_element_type=jnp.float32
        )
    result_ref[...] = (residual + (gates[0] * picked[0] + gates[1] * picked[1])).astype(
        jnp.bfloat16
    )
    grad_gates = [jnp.sum(grad_result * rows, 1, keepdims=True) for rows in picked]
    common = gates[0] * grad_gates[0] + gates[1] * grad_gates[1]
    grad_router = jnp.zeros((tokens, LANES), jnp.float32)
    for pick in range(2):
        grad_router = grad_router + jnp.where(
            picks[pick], gates[pick] * (grad_gates[pick] - common), 0.0
        )
    normed = (residual * unit(residual) * gain_ref[1:2, :]).astype(jnp.bfloat16)
    router_grad = jnp.zeros((width, LANES), jnp.float32)
    for part in split(grad_router):
        grad_normed = grad_normed + nt_dot(part, router_ref[...])
        router_grad = router_grad + tn_dot(normed, part)
    router_grad_ref[...] = router_grad
    from_norm, grad_gain = norm_back(residual, gain_ref[1:2, :], grad_normed)
    gain_grad_ref[1:2, :] = grad_gain
    grad_residual = grad_result + from_norm
    grad_residual_ref[...] = grad_residual
    branch = grad_residual.astype(jnp.bfloat16)
    branch_ref[...] = branch
    grad_mix_ref[...] = nt_dot(branch, output_ref[...]).astype(jnp.bfloat16)
    tick()

    row, column = row_iota(LANES, LANES), column_iota(LANES, LANES)
    upside = (row + column == LANES - 1).astype(jnp.float32)

    def attend_back(pair, carry):
        lanes = pl.ds(pl.multiple_of(pair * LANES, LANES), LANES)
        fill_bias(bias_ref.at[pl.ds(pair, 1)], table_ref, blocks)
        dk_sum[...] = jnp.zeros_like(dk_sum)
        dv_sum[...] = jnp.zeros_like(dv_sum)
        skew_ref[...] = jnp.zeros_like(skew_ref)
        for block in range(blocks):
            rows = pl.ds(block * LANES, LANES)
            reach = (block + 1) * LANES
            dq = jnp.zeros((LANES, LANES), jnp.float32)
            for head in range(2):
                query = only(q_ref[rows, lanes], head)
                grad = only(grad_mix_ref[rows, lanes], head)
                keys = k_ref[:reach, lanes]
                logits = masked_logits(query, keys, table_ref, head, block, length)
                exponent = jnp.exp(logits - jnp.max(logits, 1, keepdims=True))
                soft = exponent / jnp.sum(exponent, 1, keepdims=True)
                grad_soft = nt_dot(grad, v_ref[:reach, lanes])
                inner = jnp.sum(soft * grad_soft, 1, keepdims=True)
                grad_logits = (soft * (grad_soft - inner)).astype(jnp.bfloat16)
                dv_sum[:reach, :] += tn_dot(soft.astype(jnp.bfloat16), grad)
                dk_sum[:reach, :] += tn_dot(grad_logits, query)
                dq = dq + jnp.dot(
                    grad_logits, only(keys, head), preferred_element_type=jnp.float32
                )
                wide = grad_logits.astype(jnp.float32)
                for j in range(block + 1):
                    skew_ref[head, block - j] += wide[:, j * LANES : (j + 1) * LANES]
            dq_ref[rows, lanes] = (dq * scale).astype(jnp.bfloat16)
        dk_ref[:, lanes] = (dk_sum[...] * scale).astype(jnp.bfloat16)
        dv_ref[:, lanes] = dv_sum[...].astype(jnp.bfloat16)
        for head in range(2):
            for offset in range(blocks):
                flipped = jnp.dot(
                    upside,
                    skew_ref[head, offset],
                    precision=HIGH,
                    preferred_element_type=jnp.float32,
                )
                padded = jnp.concatenate([flipped, jnp.zeros_like(flipped)], 1)
                lined = pltpu.roll(padded, 0, 1, stride=1, stride_axis=0)
                diag_ref[pair, head, offset, :] = jnp.sum(lined, 0)
        return carry

    pairs = width // LANES
    lax.fori_loop(0, pairs // 2, attend_back, 0)
    tick()
    lax.fori_loop(pairs // 2, pairs, attend_back, 0)
    tick()
    grad_normed = nt_dot(dq_ref[...], query_ref[...])
    grad_normed = grad_normed + nt_dot(dk_ref[...], key_ref[...])
    grad_normed = grad_normed + nt_dot(dv_ref[...], value_ref[...])
    inputs = x_ref[...].astype(jnp.float32)
    from_norm, grad_gain = norm_back(inputs, gain_ref[0:1, :], grad_normed)
    gain_grad_ref[0:1, :] = grad_gain
    input_grad_ref[...] = (grad_residual_ref[...] + from_norm).astype(jnp.bfloat16)


def backward_kernel(experts, capacity, length_ref, *refs):
    backward_math(experts, capacity, lambda: None, length_ref[0], *refs)


VMEM = pl.BlockSpec(memory_space=pltpu.VMEM)
SMEM = pl.BlockSpec(memory_space=pltpu.SMEM)


def layer_forward(index, experts, capacity, length, x, g, routes, routes_t, weights, router, gains, bias):
    _, tokens, width = x.shape
    blocks = tokens // LANES
    flat = jax.ShapeDtypeStruct((tokens, width), jnp.bfloat16)
    rows = pl.BlockSpec((None, tokens, width), lambda i: (index, 0, 0))
    return pl.pallas_call(
        functools.partial(forward_kernel, experts, capacity),
        grid=(1,),
        out_shape=(
            jax.ShapeDtypeStruct((experts * capacity // SLOTS, 2, SLOTS, width), jnp.bfloat16),
            flat,
            flat,
            flat,
            flat,
            flat,
            jax.ShapeDtypeStruct((tokens, width), jnp.float32),
            jax.ShapeDtypeStruct((tokens, LANES), jnp.float32),
        ),
        in_specs=[SMEM, rows, rows, *([VMEM] * 9)],
        out_specs=[VMEM] * 8,
        scratch_shapes=[pltpu.VMEM((2, blocks, LANES, LANES), jnp.float32)],
        compiler_params=pltpu.CompilerParams(vmem_limit_bytes=56 * 2**20),
        cost_estimate=pl.CostEstimate(
            flops=2 * tokens * width * (4 * width + 4 * tokens + 6 * tokens),
            bytes_accessed=40 * tokens * width,
            transcendentals=tokens * tokens * 12,
        ),
        name="layer_forward",
    )(length, x, g, routes, routes_t, *weights, router, gains, bias)


def layer_backward(
    index, experts, capacity, length, x, g, routes, weights, router, gains, bias, saved, returned
):
    _, tokens, width = x.shape
    blocks = tokens // LANES
    flat = jax.ShapeDtypeStruct((tokens, width), jnp.bfloat16)
    _, count, _, slots, _ = returned.shape

    def one(array):
        return pl.BlockSpec((None, *array.shape[1:]), lambda i: (index, 0, 0))

    rows = one(x)

    def side(which):
        return pl.BlockSpec(
            (None, count, None, slots, width), lambda i: (index, 0, which, 0, 0)
        )

    return pl.pallas_call(
        functools.partial(backward_kernel, experts, capacity),
        grid=(1,),
        out_shape=(
            *([flat] * 6),
            jax.ShapeDtypeStruct((width, LANES), jnp.float32),
            jax.ShapeDtypeStruct((2, width), jnp.float32),
            jax.ShapeDtypeStruct(bias.shape, jnp.float32),
        ),
        in_specs=[
            SMEM,
            rows,
            rows,
            one(routes),
            *([VMEM] * 7),
            *map(one, saved),
            side(0),
            side(1),
        ],
        out_specs=[VMEM] * 9,
        scratch_shapes=[
            pltpu.VMEM((tokens, width), jnp.bfloat16),
            pltpu.VMEM((tokens, width), jnp.float32),
            pltpu.VMEM((2, blocks, LANES, LANES), jnp.float32),
            pltpu.VMEM((tokens, LANES), jnp.float32),
            pltpu.VMEM((tokens, LANES), jnp.float32),
            pltpu.VMEM((2, blocks, LANES, LANES), jnp.float32),
        ],
        compiler_params=pltpu.CompilerParams(vmem_limit_bytes=56 * 2**20),
        cost_estimate=pl.CostEstimate(
            flops=2 * tokens * width * (4 * width + 12 * tokens + 10 * tokens),
            bytes_accessed=40 * tokens * width,
            transcendentals=tokens * tokens * 12,
        ),
        name="layer_backward",
    )(length, x, g, routes, *weights, router, gains, bias, *saved, returned, returned)


def expert_kernel(count, x_ref, g_ref, *refs):
    inner_refs, outer_refs = refs[:count], refs[count : 2 * count]
    back_ref, hidden_ref, grad_ref = refs[2 * count :]
    shape = x_ref.shape
    inputs = x_ref[...].reshape(-1, shape[-1])
    grads = g_ref[...].reshape(-1, shape[-1])
    out = jnp.zeros(inputs.shape, jnp.float32)
    back = jnp.zeros(inputs.shape, jnp.float32)
    start = 0
    for inner_ref, outer_ref in zip(inner_refs, outer_refs):
        part = pl.ds(start, inner_ref.shape[1])
        start += inner_ref.shape[1]
        pre_act = jnp.dot(inputs, inner_ref[...], preferred_element_type=jnp.float32)
        activated, slope = gelu_parts(pre_act)
        hidden = activated.astype(jnp.bfloat16)
        grad_pre = (nt_dot(grads, outer_ref[...]) * slope).astype(jnp.bfloat16)
        hidden_ref[:, part] = hidden
        grad_ref[:, part] = grad_pre
        out = out + jnp.dot(hidden, outer_ref[...], preferred_element_type=jnp.float32)
        back = back + nt_dot(grad_pre, inner_ref[...])
    back_ref[:, 0] = out.astype(jnp.bfloat16).reshape(shape)
    back_ref[:, 1] = back.astype(jnp.bfloat16).reshape(shape)


def expert_pass(arrived, inner, outer):
    sources, _, capacity, width = arrived.shape
    total = sources * capacity
    units = sum(part.shape[1] for part in inner)
    group = sources // 4

    def side(which):
        return pl.BlockSpec((group, None, capacity, width), lambda i: (i, which, 0, 0))

    def whole(shape):
        return pl.BlockSpec(shape, lambda i: (0, 0), pipeline_mode=pl.Buffered(1))

    unit_spec = pl.BlockSpec((group * capacity, units), lambda i: (i, 0))
    deep = jax.ShapeDtypeStruct((total, units), jnp.bfloat16)
    return pl.pallas_call(
        functools.partial(expert_kernel, len(inner)),
        grid=(sources // group,),
        out_shape=(jax.ShapeDtypeStruct(arrived.shape, jnp.bfloat16), deep, deep),
        in_specs=[side(0), side(1), *(whole(part.shape) for part in (*inner, *outer))],
        out_specs=(
            pl.BlockSpec((group, 2, capacity, width), lambda i: (i, 0, 0, 0)),
            unit_spec,
            unit_spec,
        ),
        compiler_params=pltpu.CompilerParams(vmem_limit_bytes=60 * 2**20),
        cost_estimate=pl.CostEstimate(
            flops=8 * total * width * units,
            bytes_accessed=4 * (2 * width + units) * total + 4 * width * units,
            transcendentals=2 * total * units,
        ),
        name="expert_pass",
    )(arrived, arrived, *inner, *outer)


def weight_kernel(x0_ref, x1_ref, g0_ref, g1_ref, p0_ref, p1_ref, h0_ref, h1_ref, *out_refs):
    inner_ref, outer_ref = out_refs

    def flat(ref):
        return ref[...].reshape(-1, ref.shape[-1])

    inner = tn_dot(flat(x0_ref), p0_ref[...]) + tn_dot(flat(x1_ref), p1_ref[...])
    inner_ref[...] = inner.astype(jnp.bfloat16)
    outer = tn_dot(h0_ref[...], flat(g0_ref)) + tn_dot(h1_ref[...], flat(g1_ref))
    outer_ref[...] = outer.astype(jnp.bfloat16)


def weight_pass(first, count, chunks, arrived, pres, hiddens):
    sources, _, capacity, width = arrived[0].shape
    total = sources * capacity
    size = hiddens[0].shape[1] // chunks
    step = math.gcd(size, 256)
    steps = size // step

    def side(which):
        return pl.BlockSpec(
            (sources, None, capacity, width),
            lambda i: (0, which, 0, 0),
            pipeline_mode=pl.Buffered(1),
        )

    units = pl.BlockSpec((total, step), lambda i: (0, first * steps + i))
    inner, outer = pl.pallas_call(
        weight_kernel,
        grid=(count * steps,),
        out_shape=(
            jax.ShapeDtypeStruct((count, width, size), jnp.bfloat16),
            jax.ShapeDtypeStruct((count * size, width), jnp.bfloat16),
        ),
        in_specs=[side(0)] * 2 + [side(1)] * 2 + [units] * 4,
        out_specs=(
            pl.BlockSpec((None, width, step), lambda i: (i // steps, 0, i % steps)),
            pl.BlockSpec((step, width), lambda i: (i, 0)),
        ),
        compiler_params=pltpu.CompilerParams(vmem_limit_bytes=60 * 2**20),
        cost_estimate=pl.CostEstimate(
            flops=8 * total * width * count * size,
            bytes_accessed=8 * total * (width + count * size) + 4 * width * count * size,
            transcendentals=0,
        ),
        name="weight_pass",
    )(*arrived, *arrived, *pres, *hiddens)
    return list(inner), list(outer.reshape(count, size, width))


FOLD_ORDERS = (("y", "x", "zl", "zh"), ("x", "zl", "y", "zh"), ("zl", "y", "x", "zh"))


def greet(axes):
    barrier = pltpu.get_barrier_semaphore()
    for axis in axes:
        pl.semaphore_signal(
            barrier,
            inc=1,
            device_id={axis: 1 - lax.axis_index(axis)},
            device_id_type=pl.DeviceIdType.MESH,
        )
    pl.semaphore_wait(barrier, len(axes))


def push(source, target, send_sem, recv_sem, axis):
    copy = pltpu.make_async_remote_copy(
        src_ref=source,
        dst_ref=target,
        send_sem=send_sem,
        recv_sem=recv_sem,
        device_id={axis: 1 - lax.axis_index(axis)},
        device_id_type=pl.DeviceIdType.MESH,
    )
    copy.start()
    return copy


def fold_math(operands, ready_ref, outs, grads, sums, inboxes, send_sem, recv_sem):
    count = len(outs)
    grads = [*grads, ready_ref]
    mine = {axis: lax.axis_index(axis) for axis in ("core", "y", "x", "zl", "zh")}
    core = mine["core"]
    orders = [FOLD_ORDERS[i % len(FOLD_ORDERS)] for i in range(count)]

    def cut(ref, i, depth, axes, partner=None):
        done = orders[i][:depth]
        place = dict(mine)
        if partner is not None:
            place[partner] = 1 - place[partner]
        index = [place[axis] if axis in done else slice(None) for axis in axes]
        columns = slice(None)
        if "zh" in done:
            width = ref.shape[-1] // 2
            columns = pl.ds(pl.multiple_of(place["zh"] * width, LANES), width)
        return ref.at[(*index, slice(None), columns)]

    spread, joined = ("y", "x", "zl"), ("x", "zl")
    started = []
    flying = []
    for i in range(count):
        if i < count - 1:
            left_0, right_0, left_1, right_1 = operands[i]
            total = tn_dot(left_0[...], right_0[...]) + tn_dot(left_1[...], right_1[...])
            grads[i][...] = total.astype(jnp.bfloat16).reshape(grads[i].shape)
        flying.append(
            push(
                grads[i].at[:, 1 - core],
                inboxes[0][i],
                send_sem.at[i, 0],
                recv_sem.at[i, 0],
                "core",
            )
        )
    for step in range(5):
        for i in range(count):
            flying[i].wait_recv()
            if step == 0:
                sums[i][...] = (
                    grads[i][:, core].astype(jnp.float32)
                    + inboxes[0][i][...].astype(jnp.float32)
                ).astype(jnp.bfloat16)
            else:
                kept = cut(sums[i], i, step, spread)
                total = kept[...].astype(jnp.float32) + inboxes[step][i][...].astype(jnp.float32)
                kept[...] = total.astype(jnp.bfloat16)
            started.append(flying[i])
            if step < 4:
                axis = orders[i][step]
                flying[i] = push(
                    cut(sums[i], i, step + 1, spread, axis),
                    inboxes[step + 1][i],
                    send_sem.at[i, step + 1],
                    recv_sem.at[i, step + 1],
                    axis,
                )
    for i in range(count):
        cut(outs[i], i, 4, joined)[...] = cut(sums[i], i, 4, spread)[...]
    left = [[axis for axis in reversed(order)] for order in orders]
    for step in range(4):
        for i in range(count):
            if step:
                if flying[i] is not None:
                    flying[i].wait_recv()
                    started.append(flying[i])
            axis = left[i][step]
            flying[i] = None
            if axis != "y":
                place = cut(outs[i], i, 4 - step, joined)
                flying[i] = push(
                    place, place, send_sem.at[i, 5 + step], recv_sem.at[i, 5 + step], axis
                )
    for i in range(count):
        if flying[i] is not None:
            flying[i].wait_recv()
            started.append(flying[i])
    for copy in started:
        copy.wait_send()


PEER_AXES = ("y", "zl", "x")
CHUNKS = 4


def peer_of(step):
    target, block = {}, 0
    for bit, axis in enumerate(reversed(PEER_AXES)):
        place = lax.axis_index(axis)
        if step >> bit & 1:
            place = 1 - place
            target[axis] = place
        block = block + place * (1 << bit)
    return target, block


def send(source, target, send_sem, recv_sem, device):
    copy = pltpu.make_async_remote_copy(
        src_ref=source,
        dst_ref=target,
        send_sem=send_sem,
        recv_sem=recv_sem,
        device_id=device,
        device_id_type=pl.DeviceIdType.MESH,
    )
    copy.start()
    return copy


def meet(devices):
    barrier = pltpu.get_barrier_semaphore()
    for device in devices:
        pl.semaphore_signal(
            barrier, inc=1, device_id=device, device_id_type=pl.DeviceIdType.MESH
        )
    pl.semaphore_wait(barrier, len(devices))


def across(axis):
    return {axis: 1 - lax.axis_index(axis)}


def head_kernel(
    experts,
    capacity,
    lengths_ref,
    x_ref,
    g_ref,
    routes_ref,
    routes_t_ref,
    inner_ref,
    outer_ref,
    *refs,
):
    count = 6
    parts, refs = refs[:count], refs[count:]
    wholes, refs = refs[:count], refs[count:]
    inner_outs, outer_outs, refs = refs[:4], refs[4:8], refs[8:]
    arrived_ref, refs = refs[0], refs[1:]
    normed_ref, q_ref, k_ref, v_ref, mix_ref, residual_ref, gates_ref, gain_ref, bias_ref = refs[:9]
    refs = refs[9:]
    sent_refs, relays = refs[:2], refs[2:4]
    table_ref = refs[4]
    mixer_send, mixer_recv, move_send, move_recv, row_send, row_recv, local_sem = refs[5:]
    core, y, x, zh = (lax.axis_index(axis) for axis in ("core", "y", "x", "zh"))
    at_home = zh == y
    away = zh != y
    batch, tokens, width = x_ref.shape

    meet([across("core"), across("zh"), *(peer_of(step)[0] for step in range(1, 8))])

    sources = (inner_ref, outer_ref)
    outs = (inner_outs, outer_outs)
    rows = inner_ref.shape[0] // CHUNKS

    def piece(ref, chunk):
        return ref.at[pl.ds(chunk * rows, rows)]

    class Moves:
        @staticmethod
        def copy(which, chunk, kind, source, target, axis):
            return pltpu.make_async_remote_copy(
                src_ref=piece(source, chunk),
                dst_ref=piece(target, chunk),
                send_sem=move_send.at[which, chunk, kind],
                recv_sem=move_recv.at[which, chunk, kind],
                device_id=across(axis),
                device_id_type=pl.DeviceIdType.MESH,
            )

    def move_z(which, chunk):
        source = sources[which]

        @pl.when(at_home)
        def _():
            Moves.copy(which, chunk, 0, source, outs[which][0], "zh").start()

        @pl.when(away)
        def _():
            Moves.copy(which, chunk, 0, source, relays[which], "zh").start()

    def move_first(which, chunk):
        source = sources[which]

        @pl.when(away)
        def _():
            Moves.copy(which, chunk, 1, source, outs[which][2], "y").start()

        @pl.when(at_home)
        def _():
            Moves.copy(which, chunk, 2, source, outs[which][1], "core").start()

    def relay_z(which, chunk):
        @pl.when(at_home)
        def _():
            Moves.copy(which, chunk, 0, sources[which], relays[which], "zh").wait_recv()
            Moves.copy(which, chunk, 1, relays[which], outs[which][2], "y").start()

        @pl.when(away)
        def _():
            Moves.copy(which, chunk, 0, sources[which], outs[which][0], "zh").wait_recv()
            Moves.copy(which, chunk, 2, outs[which][0], outs[which][1], "core").start()

    def relay_y(which, chunk):
        Moves.copy(which, chunk, 1, sources[which], outs[which][2], "y").wait_recv()
        Moves.copy(which, chunk, 3, outs[which][2], outs[which][3], "core").start()

    def finish(which, chunk):
        for kind, axis in ((2, "core"), (3, "core")):
            Moves.copy(which, chunk, kind, sources[which], outs[which][1], axis).wait_recv()
        for kind, axis in ((0, "zh"), (1, "y"), (2, "core"), (3, "core")):
            Moves.copy(which, chunk, kind, sources[which], outs[which][1], axis).wait_send()

    def half(part, which):
        size = part.shape[0] // 2
        return pl.ds(pl.multiple_of(which * size, size), size)

    def spot(part, whole, y_at, core_at, half_at=None):
        size = part.shape[0]
        start = (y_at * 2 + core_at) * size
        if half_at is not None:
            size = size // 2
            start = start + half_at * size
        return whole.at[pl.ds(pl.multiple_of(start, size), size)]

    mixers = []
    for i, (part, whole) in enumerate(zip(parts, wholes)):
        for j, axis in enumerate(("y", "core")):
            source = part if axis == "core" else part.at[half(part, x)]
            place = spot(part, whole, y, core, x if axis == "y" else None)
            mixers.append(push(source, place, mixer_send.at[i, j], mixer_recv.at[i, j], axis))
    for chunk in range(CHUNKS):
        move_z(0, chunk)
    for i, (part, whole) in enumerate(zip(parts, wholes)):
        spot(part, whole, y, core)[...] = part[...]
    for i, whole in enumerate(wholes):
        mixers[2 * i].wait_recv()
        place = spot(parts[i], whole, 1 - y, core, x)
        for j, axis in ((2, "x"), (3, "core")):
            mixers.append(push(place, place, mixer_send.at[i, j], mixer_recv.at[i, j], axis))
    for i, whole in enumerate(wholes):
        mixers[2 * count + 2 * i].wait_recv()
        place = spot(parts[i], whole, 1 - y, core, 1 - x)
        mixers.append(push(place, place, mixer_send.at[i, 4], mixer_recv.at[i, 4], "core"))
    for which in range(2):
        for chunk in range(CHUNKS):
            move_first(which, chunk)

    @pl.when(at_home)
    def _():
        for which in range(2):
            pltpu.make_async_copy(sources[which], outs[which][0], local_sem.at[which]).start()

    for i in range(count):
        mixers[2 * i + 1].wait_recv()
        mixers[2 * count + 2 * i + 1].wait_recv()
        mixers[4 * count + i].wait_recv()

    misc = wholes[5][...].astype(jnp.float32)
    per_shard = misc.shape[0] // 4
    for i in range(2):
        line = sum(misc[s * per_shard + 3 + i : s * per_shard + 4 + i, :] for s in range(4))
        gain_ref[i : i + 1, :] = line
    for head in range(4 * 3):
        row = (head // 3) * per_shard + head % 3
        for offset in range(bias_ref.shape[2]):
            bias_ref[head // 2, head % 2, offset : offset + 1, :] = misc[
                row : row + 1, offset * 2 * LANES : (offset + 1) * 2 * LANES
            ]

    rows_flying = []
    for b in range(batch):
        forward_math(
            experts,
            capacity,
            lengths_ref[b],
            x_ref.at[b],
            g_ref.at[b],
            routes_ref.at[b],
            routes_t_ref.at[b],
            *wholes[:5],
            gain_ref,
            bias_ref,
            sent_refs[b],
            normed_ref.at[b],
            q_ref.at[b],
            k_ref.at[b],
            v_ref.at[b],
            mix_ref.at[b],
            residual_ref.at[b],
            gates_ref.at[b],
            table_ref,
        )
        _, mine = peer_of(0)
        local = pltpu.make_async_copy(
            sent_refs[b].at[mine], arrived_ref.at[b, mine], local_sem.at[2 + b]
        )
        local.start()
        rows_flying.append(local)
        for turn, step in enumerate((7, 1, 6, 2, 5, 3, 4)):
            target, block = peer_of(step)
            copy = send(
                sent_refs[b].at[block],
                arrived_ref.at[b, mine],
                row_send.at[b, step - 1],
                row_recv.at[b, step - 1],
                target,
            )
            rows_flying.append(copy)
            if b == 0 and turn % 2 == 0:
                move_z(1, turn // 2)
        if b == 0:
            for chunk in range(CHUNKS):
                relay_z(0, chunk)
    for chunk in range(CHUNKS):
        relay_y(0, chunk)
    for chunk in range(CHUNKS):
        relay_z(1, chunk)
    for chunk in range(CHUNKS):
        relay_y(1, chunk)
    for which in range(2):
        for chunk in range(CHUNKS):
            finish(which, chunk)

    @pl.when(at_home)
    def _():
        for which in range(2):
            pltpu.make_async_copy(sources[which], outs[which][0], local_sem.at[which]).wait()

    for copy in mixers:
        copy.wait_send()
    for copy in rows_flying:
        copy.wait()


def layer_head(experts, capacity, lengths, x, g, routes, routes_t, inner, outer, parts, bias_shape):
    batch, tokens, width = x.shape
    blocks = tokens // LANES
    count = len(parts)
    shape = jax.ShapeDtypeStruct
    wholes = [shape((4 * part.shape[0], part.shape[1]), part.dtype) for part in parts]
    moved = shape(inner.shape, inner.dtype)
    exchange = (experts * capacity // SLOTS, 2, SLOTS, width)
    flat = shape(x.shape, jnp.bfloat16)
    anywhere = pl.BlockSpec(memory_space=pl.ANY)
    dma = pltpu.SemaphoreType.DMA
    results = pl.pallas_call(
        functools.partial(head_kernel, experts, capacity),
        out_shape=(
            *wholes,
            *([moved] * 8),
            shape((batch, *exchange), jnp.bfloat16),
            *([flat] * 5),
            shape(x.shape, jnp.float32),
            shape((batch, tokens, LANES), jnp.float32),
            shape((2, width), jnp.float32),
            shape(bias_shape, jnp.float32),
        ),
        in_specs=[SMEM, *([VMEM] * (6 + count))],
        out_specs=[*([VMEM] * count), *([anywhere] * 9), *([VMEM] * 9)],
        scratch_shapes=[
            pltpu.VMEM(exchange, jnp.bfloat16),
            pltpu.VMEM(exchange, jnp.bfloat16),
            pltpu.VMEM(inner.shape, jnp.bfloat16),
            pltpu.VMEM(outer.shape, jnp.bfloat16),
            pltpu.VMEM((2, blocks, LANES, LANES), jnp.float32),
            dma((count, 5)),
            dma((count, 5)),
            dma((2, CHUNKS, 4)),
            dma((2, CHUNKS, 4)),
            dma((batch, 7)),
            dma((batch, 7)),
            dma((4,)),
        ],
        compiler_params=pltpu.CompilerParams(
            collective_id=1, has_side_effects=True, vmem_limit_bytes=60 * 2**20
        ),
        name="layer_head",
    )(lengths, x, g, routes, routes_t, inner, outer, *parts)
    wholes, rest = results[:count], results[count:]
    return wholes, rest[:4], rest[4:8], rest[8], rest[9:16], rest[16], rest[17]


def middle_kernel(arrived_ref, *refs):
    inner_refs, outer_refs, refs = refs[:4], refs[4:8], refs[8:]
    returned_ref, outs, refs = refs[0], refs[1:5], refs[5:]
    taken, going, inner_sums, outer_sums, refs = refs[0], refs[1], refs[2:6], refs[6:10], refs[10:]
    stage, inbox, take_sem, send_sem, recv_sem, local_sem, core_send, core_recv = refs
    y, zl, x = (lax.axis_index(axis) for axis in PEER_AXES)
    mine = y * 4 + zl * 2 + x
    batch, sources, _, slots, width = arrived_ref.shape
    groups = sources // 2
    total = batch * groups

    meet([across("core"), *(peer_of(step)[0] for step in range(1, 8))])
    for ref in (*inner_sums, *outer_sums):
        ref[...] = jnp.zeros_like(ref)

    def partner(i, side):
        turn = lax.rem(i, groups)
        step = turn if side == 0 else 2 * groups - 1 - turn
        places = {}
        for axis, place, flipped in (
            ("y", y, step // 4),
            ("zl", zl, lax.rem(step // 2, 2)),
            ("x", x, lax.rem(step, 2)),
        ):
            places[axis] = place + flipped - 2 * place * flipped
        return lax.div(i, groups), places, (places["y"] * 2 + places["zl"]) * 2 + places["x"]

    def take(i, side):
        b, _, block = partner(i, side)
        slot = lax.rem(i, 2)
        return pltpu.make_async_copy(
            arrived_ref.at[b, block], taken.at[slot, side], take_sem.at[slot, side]
        )

    def back(i, side, action):
        b, target, block = partner(i, side)
        slot = lax.rem(i, 2)

        def far():
            action(
                pltpu.make_async_remote_copy(
                    src_ref=going.at[slot, side],
                    dst_ref=returned_ref.at[b, mine],
                    send_sem=send_sem.at[b, block],
                    recv_sem=recv_sem.at[b, mine],
                    device_id=target,
                    device_id_type=pl.DeviceIdType.MESH,
                ),
                True,
            )

        if side:
            far()
            return
        pl.when(block != mine)(far)

        @pl.when(block == mine)
        def _():
            action(
                pltpu.make_async_copy(
                    going.at[slot, side], returned_ref.at[b, mine], local_sem.at[b]
                ),
                False,
            )

    def begin(copy, remote):
        copy.start()

    def sent(copy, remote):
        if remote:
            copy.wait_send()
        else:
            copy.wait()

    for side in range(2):
        take(0, side).start()

    def work(i, carry):
        slot = lax.rem(i, 2)

        @pl.when(i + 1 < total)
        def _():
            for side in range(2):
                take(i + 1, side).start()

        for side in range(2):
            take(i, side).wait()
        rows = taken[slot, :, 0].reshape(2 * slots, width)
        grads = taken[slot, :, 1].reshape(2 * slots, width)
        out = jnp.zeros((2 * slots, width), jnp.float32)
        result = jnp.zeros((2 * slots, width), jnp.float32)
        for part in range(4):
            inner, outer = inner_refs[part][...], outer_refs[part][...]
            pre_act = jnp.dot(rows, inner, preferred_element_type=jnp.float32)
            activated, slope = gelu_parts(pre_act)
            hidden = activated.astype(jnp.bfloat16)
            grad_pre = (nt_dot(grads, outer) * slope).astype(jnp.bfloat16)
            out = out + jnp.dot(hidden, outer, preferred_element_type=jnp.float32)
            result = result + nt_dot(grad_pre, inner)
            inner_sums[part][...] += tn_dot(rows, grad_pre)
            outer_sums[part][...] += tn_dot(hidden, grads)

        @pl.when(i >= 2)
        def _():
            for side in range(2):
                back(i - 2, side, sent)

        going[slot, :, 0] = out.astype(jnp.bfloat16).reshape(2, slots, width)
        going[slot, :, 1] = result.astype(jnp.bfloat16).reshape(2, slots, width)
        for side in range(2):
            back(i, side, begin)
        return carry

    lax.fori_loop(0, total, work, 0)
    crossing = []
    for index in range(4):
        sums = (inner_sums, outer_sums)[index % 2]
        stage[index] = sums[3 - 2 * (index // 2)][...].astype(jnp.bfloat16)
        crossing.append(
            send(
                stage.at[index],
                inbox.at[index],
                core_send.at[index],
                core_recv.at[index],
                across("core"),
            )
        )
    for index in range(4):
        sums = (inner_sums, outer_sums)[index % 2]
        crossing[index].wait()
        met = sums[2 - 2 * (index // 2)][...] + inbox[index].astype(jnp.float32)
        outs[index][...] = met.astype(jnp.bfloat16)
    for i in (total - 2, total - 1):
        for side in range(2):
            back(i, side, sent)
    for b in range(batch):
        for step in range(1, 8):
            target, block = peer_of(step)
            pltpu.make_async_remote_copy(
                src_ref=going.at[0, 0],
                dst_ref=returned_ref.at[b, block],
                send_sem=send_sem.at[b, block],
                recv_sem=recv_sem.at[b, block],
                device_id=target,
                device_id_type=pl.DeviceIdType.MESH,
            ).wait_recv()


def layer_middle(arrived, inner, outer):
    batch, sources, _, slots, width = arrived.shape
    quarter = inner[0].shape
    anywhere = pl.BlockSpec(memory_space=pl.ANY)
    dma = pltpu.SemaphoreType.DMA
    results = pl.pallas_call(
        middle_kernel,
        out_shape=(
            jax.ShapeDtypeStruct(arrived.shape, jnp.bfloat16),
            *([jax.ShapeDtypeStruct(quarter, jnp.bfloat16)] * 4),
        ),
        in_specs=[anywhere, *([VMEM] * 8)],
        out_specs=[anywhere, *([VMEM] * 4)],
        scratch_shapes=[
            pltpu.VMEM((2, 2, 2, slots, width), jnp.bfloat16),
            pltpu.VMEM((2, 2, 2, slots, width), jnp.bfloat16),
            *([pltpu.VMEM(quarter, jnp.float32)] * 8),
            pltpu.VMEM((4, *quarter), jnp.bfloat16),
            pltpu.VMEM((4, *quarter), jnp.bfloat16),
            dma((2, 2)),
            dma((batch, sources)),
            dma((batch, sources)),
            dma((batch,)),
            dma((4,)),
            dma((4,)),
        ],
        compiler_params=pltpu.CompilerParams(
            collective_id=3, has_side_effects=True, vmem_limit_bytes=63 * 2**20
        ),
        name="layer_middle",
    )(arrived, *inner, *outer)
    return results[0], results[1:]


def bias_columns(diagonals, shards, bucket_count):
    lines = diagonals.shape[1]
    width = lines
    row = row_iota(lines, 1)
    distance = (row // (2 * LANES)) * LANES + LANES - 1 - row % (2 * LANES)
    table = bucket_table(lines // (2 * LANES) * LANES)
    bucket = jnp.minimum(distance, 16)
    for value in range(17, bucket_count):
        bucket = bucket + (distance >= int(np.argmax(table >= value))).astype(jnp.int32)
    lane = column_iota(1, width)
    place = lane % (width // shards)
    heads = 3
    hot = one_hot((bucket == place % bucket_count) & (place < heads * bucket_count))
    sums = sum(jnp.dot(part, hot, preferred_element_type=jnp.float32) for part in split(diagonals))
    head = lane // (width // shards) * heads + place // bucket_count
    return jnp.sum(jnp.where(row_iota(sums.shape[0], width) == head, sums, 0.0), 0, keepdims=True)


def tail_kernel(experts, capacity, bucket_count, lengths_ref, *refs):
    x_ref, g_ref, routes_ref, refs = refs[0], refs[1], refs[2], refs[3:]
    weights, gain_ref, bias_ref, refs = refs[:5], refs[5], refs[6], refs[7:]
    normed_ref, q_ref, k_ref, v_ref, mix_ref, residual_ref, gates_ref, returned_ref = refs[:8]
    partials, refs = refs[8:12], refs[12:]
    result_ref, input_grad_ref, home_refs, outs, refs = refs[0], refs[1], refs[2:4], refs[4:9], refs[9:]
    out_rows, back_rows, branch, dq, dk, dv, router_grad, gain_grad, diag, refs = *refs[:9], refs[9:]
    scratch, ready, grads, sums, refs = refs[:6], refs[6], refs[7:11], refs[11:16], refs[16:]
    inboxes, refs = [refs[5 * i : 5 * i + 5] for i in range(5)], refs[25:]
    fetched, landed, fold_send, fold_recv, move_send, move_recv, local_sem, own_sem = refs
    y, zh = lax.axis_index("y"), lax.axis_index("zh")
    at_home, away = zh == y, zh != y
    batch, tokens, width = x_ref.shape
    far, near = partials[:2], partials[2:]
    rows = far[0].shape[0] // CHUNKS

    greet(("core", "y", "x", "zl", "zh"))

    def load(b):
        return [
            pltpu.make_async_copy(returned_ref.at[b, :, which], target, local_sem.at[which])
            for which, target in enumerate((out_rows, back_rows))
        ]

    def piece(ref, chunk):
        return ref.at[pl.ds(chunk * rows, rows)]

    def own(which, chunk):
        return pltpu.make_async_copy(
            piece(near[which], chunk),
            (out_rows, back_rows)[which].at[chunk],
            own_sem.at[which, chunk],
        )

    def copy(which, chunk, kind, source, target, axis):
        return pltpu.make_async_remote_copy(
            src_ref=piece(source, chunk),
            dst_ref=piece(target, chunk),
            send_sem=move_send.at[which, chunk, kind],
            recv_sem=move_recv.at[which, chunk, kind],
            device_id=across(axis),
            device_id_type=pl.DeviceIdType.MESH,
        )

    order = [(which, chunk) for which in range(2) for chunk in range(CHUNKS)]
    for which, chunk in order:
        copy(which, chunk, 0, far[which], fetched.at[which], "y").start()

        @pl.when(away)
        def _():
            copy(which, chunk, 1, near[which], landed.at[which], "zh").start()

    waiting = list(order)

    def tick(amount=2):
        for which, chunk in waiting[:amount]:
            copy(which, chunk, 0, far[which], fetched.at[which], "y").wait_recv()

            @pl.when(at_home)
            def _():
                copy(which, chunk, 1, fetched.at[which], landed.at[which], "zh").start()

        del waiting[:amount]

    for part in load(0):
        part.start()
    for b in range(batch):
        for part in load(b):
            part.wait()

        def combined():
            if b + 1 < batch:
                for part in load(b + 1):
                    part.start()
            else:
                for which, chunk in order:
                    own(which, chunk).start()
            tick(1)

        backward_math(
            experts,
            capacity,
            Ticks([combined, tick, tick]),
            lengths_ref[b],
            x_ref.at[b],
            g_ref.at[b],
            routes_ref.at[b],
            *weights,
            gain_ref,
            bias_ref,
            q_ref.at[b],
            k_ref.at[b],
            v_ref.at[b],
            residual_ref.at[b],
            gates_ref.at[b],
            out_rows,
            back_rows,
            result_ref.at[b],
            input_grad_ref.at[b],
            branch.at[b],
            dq.at[b],
            dk.at[b],
            dv.at[b],
            router_grad.at[b],
            gain_grad.at[b],
            diag.at[b],
            *scratch,
        )
    tick(len(order))

    lines = [
        jnp.concatenate(
            [
                jnp.concatenate(
                    [
                        diag[0, head // 2, head % 2, offset : offset + 1, :]
                        + diag[1, head // 2, head % 2, offset : offset + 1, :]
                        for offset in range(diag.shape[3])
                    ],
                    1,
                )
                for head in range(2 * diag.shape[1])
            ],
            0,
        )
    ]
    lines.append(jnp.zeros((16 - lines[0].shape[0], lines[0].shape[1]), jnp.float32))
    bias_line = bias_columns(jnp.concatenate(lines, 0), 4, bucket_count)
    gain_lines = gain_grad[0] + gain_grad[1]
    row = row_iota(LANES, width)
    stacked = jnp.where(
        row == 0,
        gain_lines[0:1, :],
        jnp.where(row == 1, gain_lines[1:2, :], jnp.where(row == 2, bias_line, 0.0)),
    )
    packed = jnp.concatenate([router_grad[0] + router_grad[1], stacked.T], 1)
    ready[...] = packed.astype(jnp.bfloat16).reshape(ready.shape)
    fold_math(
        [
            (normed_ref.at[0], dq.at[0], normed_ref.at[1], dq.at[1]),
            (normed_ref.at[0], dk.at[0], normed_ref.at[1], dk.at[1]),
            (normed_ref.at[0], dv.at[0], normed_ref.at[1], dv.at[1]),
            (mix_ref.at[0], branch.at[0], mix_ref.at[1], branch.at[1]),
        ],
        ready,
        outs,
        grads,
        sums,
        inboxes,
        fold_send,
        fold_recv,
    )

    for which, chunk in order:
        own(which, chunk).wait()
        copy(which, chunk, 1, near[which], landed.at[which], "zh").wait()
        copy(which, chunk, 0, far[which], fetched.at[which], "y").wait_send()
        place = pl.ds(chunk * rows, rows)

        def settle(kept):
            total = kept.astype(jnp.float32) + landed[which, place].astype(jnp.float32)
            home_refs[which][place] = total.astype(jnp.bfloat16)

        pl.when(at_home)(lambda: settle((out_rows, back_rows)[which][chunk]))
        pl.when(away)(lambda: settle(fetched[which, place]))


class Ticks:
    def __init__(self, actions):
        self.actions = list(actions)

    def __call__(self):
        self.actions.pop(0)()


def layer_tail(experts, capacity, bucket_count, lengths, x, g, routes, weights, gains, bias, saved, returned, partials):
    batch, tokens, width = x.shape
    blocks = tokens // LANES
    shape, dma = jax.ShapeDtypeStruct, pltpu.SemaphoreType.DMA
    anywhere = pl.BlockSpec(memory_space=pl.ANY)
    flat = shape(x.shape, jnp.bfloat16)
    quarter = partials[0].shape
    sizes = [(width // 16, width)] * 4 + [(width // 16, 2 * LANES)]
    boxes = []
    for depth in range(5):
        for i, (part, columns) in enumerate(sizes):
            done = FOLD_ORDERS[i % len(FOLD_ORDERS)][:depth]
            lead = [2] * (3 - sum(axis != "zh" for axis in done))
            boxes.append(
                pltpu.VMEM(
                    (*lead, part, columns // 2 if "zh" in done else columns), jnp.bfloat16
                )
            )
    side = returned.shape[1:2] + returned.shape[3:]
    results = pl.pallas_call(
        functools.partial(tail_kernel, experts, capacity, bucket_count),
        out_shape=(
            flat,
            flat,
            *([shape(quarter, jnp.bfloat16)] * 2),
            *(shape((2, 2, *size), jnp.bfloat16) for size in sizes),
        ),
        in_specs=[SMEM, *([VMEM] * (3 + 5 + 2 + 7)), *([anywhere] * 5)],
        out_specs=[VMEM] * 9,
        scratch_shapes=[
            pltpu.VMEM(side, jnp.bfloat16),
            pltpu.VMEM(side, jnp.bfloat16),
            *([pltpu.VMEM(x.shape, jnp.bfloat16)] * 4),
            pltpu.VMEM((batch, width, LANES), jnp.float32),
            pltpu.VMEM((batch, 2, width), jnp.float32),
            pltpu.VMEM((batch, *bias.shape), jnp.float32),
            pltpu.VMEM((tokens, width), jnp.bfloat16),
            pltpu.VMEM((tokens, width), jnp.float32),
            pltpu.VMEM((2, blocks, LANES, LANES), jnp.float32),
            pltpu.VMEM((tokens, LANES), jnp.float32),
            pltpu.VMEM((tokens, LANES), jnp.float32),
            pltpu.VMEM((2, blocks, LANES, LANES), jnp.float32),
            pltpu.VMEM((2, 2, 2, 2, *sizes[-1]), jnp.bfloat16),
            *(pltpu.VMEM((2, 2, 2, 2, *size), jnp.bfloat16) for size in sizes[:-1]),
            *(pltpu.VMEM((2, 2, 2, *size), jnp.bfloat16) for size in sizes),
            *boxes,
            pltpu.VMEM((2, *quarter), jnp.bfloat16),
            pltpu.VMEM((2, *quarter), jnp.bfloat16),
            dma((5, 9)),
            dma((5, 9)),
            dma((2, CHUNKS, 2)),
            dma((2, CHUNKS, 2)),
            dma((2,)),
            dma((2, CHUNKS)),
        ],
        compiler_params=pltpu.CompilerParams(
            collective_id=2, has_side_effects=True, vmem_limit_bytes=63 * 2**20
        ),
        name="layer_tail",
    )(lengths, x, g, routes, *weights, gains, bias, *saved, returned, *partials)
    folded = [out.reshape(-1, out.shape[-1]).astype(jnp.float32) for out in results[4:]]
    homes = [home.astype(jnp.float32) for home in results[2:4]]
    return results[0], results[1], folded, homes


class Grouped:
    swap_axes = "expert"

    def begin(self, sizes, lengths, x, g, routes, routes_t, inner, outer, parts, bias_shape):
        wholes = [lax.all_gather(part, "shard", axis=0, tiled=True) for part in parts]
        misc = wholes[5].reshape(-1, *parts[5].shape).astype(jnp.float32)
        gains = jnp.sum(misc[:, -2:], 0)
        bias_rows = misc[:, :-2].reshape(bias_shape)
        inner, outer = (list(lax.all_gather(part, "shard", axis=0)) for part in (inner, outer))
        arrived, saved = [], []
        for index in range(x.shape[0]):
            sent, *kept = layer_forward(
                index,
                *sizes,
                lengths[index : index + 1],
                x,
                g,
                routes[index],
                routes_t[index],
                wholes[:4],
                wholes[4],
                gains,
                bias_rows,
            )
            saved.append(kept)
            arrived.append(self.swap(sent))
        saved = [jnp.stack(pair) for pair in zip(*saved)]
        return wholes, inner, outer, arrived, saved, gains, bias_rows

    def swap(self, blocks):
        experts = lax.axis_size("expert")
        count, _, slots, width = blocks.shape
        merged = blocks.swapaxes(0, 1).reshape(2, experts, -1, width).swapaxes(0, 1)
        merged = lax.all_to_all(merged, "expert", split_axis=0, concat_axis=0, tiled=True)
        return merged.swapaxes(0, 1).reshape(2, count, slots, width).swapaxes(0, 1)

    def finish(
        self,
        sizes,
        bucket_count,
        lengths,
        x,
        g,
        routes,
        wholes,
        gains,
        bias_rows,
        saved,
        arrived,
        inner,
        outer,
        likes,
    ):
        returned, units = [], []
        for rows in arrived:
            going, *unit_pair = expert_pass(rows, inner, outer)
            units.append(unit_pair)
            returned.append(self.swap(going))
        returned = jnp.stack(returned)
        hiddens, pres = zip(*units)
        chunks = len(inner)
        passes = weight_pass(0, chunks, chunks, arrived, pres, hiddens)
        homes = [
            lax.psum_scatter(jnp.stack(grads), "shard", scatter_dimension=0).astype(jnp.float32)
            for grads in passes
        ]
        normed, queries, key_rows, value_rows, mixture, residual, gates = saved
        results, input_grads, grads, small = [], [], [], []
        for index in range(x.shape[0]):
            result, input_grad, branch, dq, dk, dv, *rest = layer_backward(
                index,
                *sizes,
                lengths[index : index + 1],
                x,
                g,
                routes,
                wholes[:4],
                wholes[4],
                gains,
                bias_rows,
                (queries, key_rows, value_rows, residual, gates),
                returned,
            )
            results.append(result)
            input_grads.append(input_grad)
            lefts = (normed[index],) * 3 + (mixture[index],)
            grads.append([tn_dot(*pair) for pair in zip(lefts, (dq, dk, dv, branch))])
            small.append(rest)
        router_grad, gain_grad, diagonals = (sum(parts) for parts in zip(*small))
        bias_grad = jnp.dot(
            diagonals.reshape(bias_rows.shape[0] * 2, -1),
            jnp.asarray(collect_hot(x.shape[1], bucket_count)),
            precision=HIGH,
        )
        small = (router_grad[:, : sizes[0]], gain_grad[0], gain_grad[1], bias_grad)
        shares = [
            lax.psum_scatter(
                sum(pair).astype(jnp.bfloat16), "shard", scatter_dimension=0, tiled=True
            ).astype(jnp.float32)
            for pair in (*zip(*grads), *((part,) for part in small))
        ]
        return jnp.stack(results), jnp.stack(input_grads), lax.psum(shares, "expert"), homes

    def shard_index(self):
        return lax.axis_index("shard")


class Halved:
    swap_axes = ("y", "zl", "x")

    def begin(self, sizes, lengths, x, g, routes, routes_t, inner, outer, parts, bias_shape):
        misc = jnp.pad(parts[5], ((0, 32 - parts[5].shape[0]), (0, 0)))
        return layer_head(
            *sizes, lengths, x, g, routes, routes_t, inner, outer, [*parts[:5], misc], bias_shape
        )

    def shard_index(self):
        return lax.axis_index("y") * 2 + lax.axis_index("core")

    def finish(
        self,
        sizes,
        bucket_count,
        lengths,
        x,
        g,
        routes,
        wholes,
        gains,
        bias_rows,
        saved,
        arrived,
        inner,
        outer,
        likes,
    ):
        returned, partials = layer_middle(arrived, inner, outer)
        result, input_grad, folded, homes = layer_tail(
            *sizes,
            bucket_count,
            lengths,
            x,
            g,
            routes,
            wholes[:5],
            gains,
            bias_rows,
            saved,
            returned,
            partials,
        )
        *large, packed = folded
        router, gain_one, gain_two, bias = likes
        small = [
            packed[:, : router.shape[1]],
            packed[:, LANES],
            packed[:, LANES + 1],
            packed[: bias.size, LANES + 2].reshape(bias.shape),
        ]
        return result, input_grad, [*large, *small], homes


def body(
    plan,
    tokens,
    cotangent,
    lengths,
    dealing,
    routes,
    query_weight,
    key_weight,
    value_weight,
    output_weight,
    router_weight,
    first_gain,
    second_gain,
    position_bias,
    inner_weight,
    outer_weight,
):
    batch, seq_len, model_width = tokens.shape
    experts = lax.axis_size(plan.swap_axes)
    capacity = 4 * seq_len // experts
    bucket_count = position_bias.shape[1]
    shard_rows = query_weight.shape[0]
    shards = model_width // shard_rows
    small_shard = (router_weight, first_gain, second_gain, position_bias)
    lane_shard = jnp.arange(model_width) // shard_rows
    bias_shard = jnp.dot(
        position_bias.astype(jnp.float32),
        jnp.asarray(spread_hot(seq_len, bucket_count)),
        precision=HIGH,
    ).astype(jnp.bfloat16)
    gain_shard = jnp.where(
        lane_shard == plan.shard_index(),
        jnp.tile(jnp.stack([first_gain, second_gain]), (1, shards)),
        0,
    )
    parts = [
        query_weight,
        key_weight,
        value_weight,
        output_weight,
        jnp.pad(router_weight, ((0, 0), (0, LANES - experts))),
        jnp.concatenate([bias_shard, gain_shard], 0),
    ]
    heads = shards * position_bias.shape[0]
    bias_shape = (heads // 2, 2, seq_len // LANES, 2 * LANES)
    seq_numbers = jnp.arange(lengths.shape[0], dtype=jnp.int32)
    seq_lengths = jnp.sum(jnp.where(seq_numbers == dealing[:, None], lengths, 0), 1)
    sizes = (experts, capacity)
    wholes, inner_parts, outer_parts, arrived, saved, gains, bias_rows = plan.begin(
        sizes,
        seq_lengths,
        tokens,
        cotangent,
        routes,
        routes.swapaxes(1, 2),
        inner_weight[0],
        outer_weight[0],
        parts,
        bias_shape,
    )
    results, input_grads, large_and_small, homes = plan.finish(
        sizes,
        bucket_count,
        seq_lengths,
        tokens,
        cotangent,
        routes,
        wholes,
        gains,
        bias_rows,
        saved,
        arrived,
        inner_parts,
        outer_parts,
        small_shard,
    )
    return (results, input_grads, *large_and_small, homes[0][None], homes[1][None])


def solution(mesh):
    experts, shards = mesh.shape["expert"], mesh.shape["shard"]
    if (experts, shards) == (8, 4):
        plan = Halved()
        mesh = jax.sharding.Mesh(
            mesh.devices.reshape(2, 2, 2, 2, 2), ("zh", "zl", "x", "y", "core")
        )
        expert_axes, shard_axes = ("zh", "zl", "x"), ("y", "core")
    else:
        plan = Grouped()
        expert_axes, shard_axes = ("expert",), ("shard",)
    both = (*expert_axes, *shard_axes)
    rows = P(both, None, None)
    weight = P(shard_axes, None)
    in_specs = (rows, rows, P(), P(both), rows, *([weight] * 5))
    in_specs += (P(shard_axes), P(shard_axes), weight)
    in_specs += (P(expert_axes, None, shard_axes), P(expert_axes, shard_axes, None))
    out_specs = (rows, rows, *([weight] * 5), P(shard_axes), P(shard_axes), weight)
    out_specs += (P(expert_axes, None, shard_axes), P(expert_axes, shard_axes, None))
    return jax.shard_map(
        functools.partial(body, plan),
        mesh=mesh,
        in_specs=in_specs,
        out_specs=out_specs,
        check_vma=False,
    )
```

profile of v0, /device:TPU:0, one launch (start us, length us, event | category | flops | bytes accessed | tf_op | source)
XLA Modules:
  0.0 521.4 jit_solution(9365468178549659942)
XLA Ops:
  0.6 0.0 copy-start
  0.7 1.4 fusion.8.lengths_ref
  2.0 0.7 stack.9
  2.7 0.7 stack.10
  3.4 0.1 tile.10
  3.5 0.0 copy-done
  3.5 1.0 fusion
  4.6 0.6 fusion.3.refs_5_
  5.2 0.8 copy.40
  6.0 0.6 pad.8.refs_4_
  6.7 1.6 copy.42.routes_ref.refs_2_
  8.3 203.0 %layer_head.1 = (bf16[768,768]{1,0:T(8,128)(2,1)}, bf16[768,768]{1,0:T(8,128)(2,1)}, bf16[768,768]{1,0:T(8,128)(2,1)}, bf16[768,768]{1,0:T(8,128)(2,1)}, bf16[76...) custom-call(s32[2]{0:T(128)} %fusion.8.lengths_ref, ...), custom_call_target="tpu_custom_call" | custom-call | tf_op jit(solution)/shard_map/layer_head/pallas_call | solution.py:978
  211.2 131.2 %layer_middle.1 = (bf16[2,8,2,192,768]{4,3,2,1,0:T(8,128)(2,1)}, bf16[768,768]{1,0:T(8,128)(2,1)}, bf16[768,768]{1,0:T(8,128)(2,1)}, bf16[768,768]{1,0:T(8,128)(2,1)}, bf16[768,768]{1,0:T(8,128)(2,1)}) custom-call(bf16[2,8,2,192,768]{4,3,2,1,0:T(8,128)(2,1)} %get-tuple-element.63.arrived_ref, bf16[768,768]{1,0:T(8,128)(2,1)} %get-tuple-element.64.refs_0_, ...), custom_call_target="tpu_custom_call" | custom-call | tf_op jit(solution)/shard_map/layer_middle/pallas_call | solution.py:1168
  342.5 166.4 %layer_tail.1 = (bf16[2,384,768]{2,1,0:T(8,128)(2,1)}, bf16[2,384,768]{2,1,0:T(8,128)(2,1)}, bf16[768,768]{1,0:T(8,128)(2,1)}, bf16[768,768]{1,0:T(8,128)(2,1)},...) custom-call(s32[2]{0:T(128)} %fusion.8.lengths_ref, ...), custom_call_target="tpu_custom_call" | custom-call | tf_op jit(solution)/shard_map/layer_tail/pallas_call | solution.py:1409
  508.9 0.0 copy-start.8
  508.9 1.0 bitcast_convert_fusion.6
  509.9 0.2 slice_reduce_fusion
  510.1 0.7 reshape_squeeze.3
  510.8 0.7 copy.47
  511.4 0.1 fusion.9
  511.5 0.6 copy.49
  512.2 0.6 copy.48
  512.8 0.0 copy-done.8
  512.8 1.1 bitcast_convert_fusion.4
  513.9 0.0 copy-done.7
  513.9 1.1 bitcast_convert_fusion.2
  515.1 0.6 copy-done.2
  515.7 2.5 bitcast_convert_fusion
  518.3 1.0 copy.54
  519.3 0.7 copy-done.4
  520.0 1.0 copy.55
  521.0 0.0 copy-done.1
  (17 shorter events, 0.1 us)
Async XLA Ops:
  0.6 2.9 copy-start
  508.9 3.9 copy-start.8
  508.9 3.9 copy-start.9
  511.4 2.5 copy-start.6
  511.4 2.5 copy-start.7
  512.8 2.3 copy-start.3
  513.9 1.8 copy-start.2
  515.7 2.5 copy-start.5
  518.3 1.7 copy-start.4
  518.3 2.7 copy-start.1
where the time goes:
time: 529 us; the launch traced here: 521 us
  Pallas kernels  501 us (95%)
  local copies, waits for them, and re-layouts  10.8 us (2%)
  other arithmetic  7.8 us (1%)
    pallas_call x1, Pallas kernels, layer_head(): pl.pallas_call(functools.partial(head_kernel, experts, capacity), out_sha...  203 us
    pallas_call x1, Pallas kernels, layer_tail(): pl.pallas_call(functools.partial(tail_kernel, experts, capacity, bucket_c...  166 us
    pallas_call x1, Pallas kernels, layer_middle(): pl.pallas_call(middle_kernel, out_shape=(jax.ShapeDtypeStruct(arrived.sha...  131 us

commit v1 on v0

--- a/solution.py
+++ b/solution.py
@@ -141,13 +141,9 @@
 
 
 def forward_math(
-    experts,
-    capacity,
     length,
     x_ref,
-    g_ref,
     routes_ref,
-    routes_t_ref,
     query_ref,
     key_ref,
     value_ref,
@@ -155,7 +151,7 @@
     router_ref,
     gain_ref,
     bias_ref,
-    sent_ref,
+    tokens_ref,
     normed_ref,
     q_ref,
     k_ref,
@@ -207,6 +203,7 @@
     )
     residual_ref[...] = residual
     normed = (residual * unit(residual) * gain_ref[1:2, :]).astype(jnp.bfloat16)
+    tokens_ref[...] = normed
     router = jnp.dot(normed, router_ref[...], preferred_element_type=jnp.float32)
     lane = column_iota(tokens, LANES)
     chosen = [
@@ -218,23 +215,41 @@
     total = gates[0] + gates[1]
     gates = [value / total for value in gates]
     gates_ref[...] = jnp.where(lane == 0, gates[0], jnp.where(lane == 1, gates[1], 0.0))
-    grads = [(g_ref[...].astype(jnp.float32) * gate).astype(jnp.bfloat16) for gate in gates]
+
+
+def dispatcher(experts, capacity, tokens_ref, g_ref, gates_ref, routes_t_ref):
+    tokens = tokens_ref.shape[0]
     places = row_places(routes_t_ref, experts, capacity)
-    slots = sent_ref.shape[2]
-    for index in range(sent_ref.shape[0]):
+    grads = [
+        (g_ref[...].astype(jnp.float32) * gates_ref[:, pick : pick + 1]).astype(jnp.bfloat16)
+        for pick in range(2)
+    ]
+
+    def fill(index, block_ref):
+        slots = block_ref.shape[1]
         slot = (row_iota(slots, tokens) + index * slots).astype(jnp.float32)
         hot = [jnp.where(slot == place, 1.0, 0.0) for place in places]
-        sent_ref[index, 0] = jnp.dot(
-            (hot[0] + hot[1]).astype(jnp.bfloat16), normed, preferred_element_type=jnp.float32
+        block_ref[0] = jnp.dot(
+            (hot[0] + hot[1]).astype(jnp.bfloat16),
+            tokens_ref[...],
+            preferred_element_type=jnp.float32,
         ).astype(jnp.bfloat16)
-        sent_ref[index, 1] = (
+        block_ref[1] = (
             jnp.dot(hot[0].astype(jnp.bfloat16), grads[0], preferred_element_type=jnp.float32)
             + jnp.dot(hot[1].astype(jnp.bfloat16), grads[1], preferred_element_type=jnp.float32)
         ).astype(jnp.bfloat16)
 
-
-def forward_kernel(experts, capacity, length_ref, *refs):
-    forward_math(experts, capacity, length_ref[0], *refs)
+    return fill
+
+
+def forward_kernel(experts, capacity, length_ref, x_ref, g_ref, routes_ref, routes_t_ref, *refs):
+    refs, (sent_ref, *outs, gates_ref, tokens_ref, table_ref) = refs[:7], refs[7:]
+    forward_math(
+        length_ref[0], x_ref, routes_ref, *refs, tokens_ref, *outs, gates_ref, table_ref
+    )
+    fill = dispatcher(experts, capacity, tokens_ref, g_ref, gates_ref, routes_t_ref)
+    for index in range(sent_ref.shape[0]):
+        fill(index, sent_ref.at[index])
 
 
 def split(value):
@@ -251,11 +266,159 @@
     return scale * (grad_unit - rows * mean), grad_gain
 
 
-def backward_math(
+def combine_math(
     experts,
     capacity,
-    tick,
+    g_ref,
+    routes_ref,
+    output_ref,
+    router_ref,
+    gain_ref,
+    residual_ref,
+    gates_ref,
+    out_rows_ref,
+    back_rows_ref,
+    result_ref,
+    branch_ref,
+    router_grad_ref,
+    gain_grad_ref,
+    grad_mix_ref,
+    grad_residual_ref,
+):
+    tokens, width = g_ref.shape
+    grad_result = g_ref[...].astype(jnp.float32)
+    residual = residual_ref[...]
+    places, picks = column_places(routes_ref, experts, capacity)
+    gates = [gates_ref[:, pick : pick + 1] for pick in range(2)]
+    slots = out_rows_ref.shape[1]
+    picked = [jnp.zeros((tokens, width), jnp.float32) for _ in range(2)]
+    grad_normed = jnp.zeros((tokens, width), jnp.float32)
+    for index in range(0, out_rows_ref.shape[0], 2):
+        slot = (column_iota(tokens, 2 * slots) + index * slots).astype(jnp.float32)
+        hot = [jnp.where(slot == place, 1.0, 0.0) for place in places]
+        out_rows = out_rows_ref[index : index + 2].reshape(2 * slots, width)
+        back_rows = back_rows_ref[index : index + 2].reshape(2 * slots, width)
+        for pick in range(2):
+            picked[pick] = picked[pick] + jnp.dot(
+                hot[pick].astype(jnp.bfloat16), out_rows, preferred_element_type=jnp.float32
+            )
+        grad_normed = grad_normed + jnp.dot(
+            (hot[0] + hot[1]).astype(jnp.bfloat16), back_rows, preferred_element_type=jnp.float32
+        )
+    result_ref[...] = (residual + (gates[0] * picked[0] + gates[1] * picked[1])).astype(
+        jnp.bfloat16
+    )
+    grad_gates = [jnp.sum(grad_result * rows, 1, keepdims=True) for rows in picked]
+    common = gates[0] * grad_gates[0] + gates[1] * grad_gates[1]
+    grad_router = jnp.zeros((tokens, LANES), jnp.float32)
+    for pick in range(2):
+        grad_router = grad_router + jnp.where(
+            picks[pick], gates[pick] * (grad_gates[pick] - common), 0.0
+        )
+    normed = (residual * unit(residual) * gain_ref[1:2, :]).astype(jnp.bfloat16)
+    router_grad = jnp.zeros((width, LANES), jnp.float32)
+    for part in split(grad_router):
+        grad_normed = grad_normed + nt_dot(part, router_ref[...])
+        router_grad = router_grad + tn_dot(normed, part)
+    router_grad_ref[...] = router_grad
+    from_norm, grad_gain = norm_back(residual, gain_ref[1:2, :], grad_normed)
+    gain_grad_ref[1:2, :] = grad_gain
+    grad_residual = grad_result + from_norm
+    grad_residual_ref[...] = grad_residual
+    branch = grad_residual.astype(jnp.bfloat16)
+    branch_ref[...] = branch
+    grad_mix_ref[...] = nt_dot(branch, output_ref[...]).astype(jnp.bfloat16)
+
+
+def attend_back_math(
+    pair,
     length,
+    q_ref,
+    k_ref,
+    v_ref,
+    grad_mix_ref,
+    bias_ref,
+    dq_ref,
+    dk_ref,
+    dv_ref,
+    diag_ref,
+    table_ref,
+    dk_sum,
+    dv_sum,
+    skew_ref,
+):
+    blocks = q_ref.shape[0] // LANES
+    scale = (LANES // 2) ** (-0.5)
+    upside = (row_iota(LANES, LANES) + column_iota(LANES, LANES) == LANES - 1).astype(jnp.float32)
+    lanes = pl.ds(pl.multiple_of(pair * LANES, LANES), LANES)
+    fill_bias(bias_ref.at[pl.ds(pair, 1)], table_ref, blocks)
+    dk_sum[...] = jnp.zeros_like(dk_sum)
+    dv_sum[...] = jnp.zeros_like(dv_sum)
+    skew_ref[...] = jnp.zeros_like(skew_ref)
+    for block in range(blocks):
+        rows = pl.ds(block * LANES, LANES)
+        reach = (block + 1) * LANES
+        dq = jnp.zeros((LANES, LANES), jnp.float32)
+        for head in range(2):
+            query = only(q_ref[rows, lanes], head)
+            grad = only(grad_mix_ref[rows, lanes], head)
+            keys = k_ref[:reach, lanes]
+            logits = masked_logits(query, keys, table_ref, head, block, length)
+            exponent = jnp.exp(logits - jnp.max(logits, 1, keepdims=True))
+            soft = exponent / jnp.sum(exponent, 1, keepdims=True)
+            grad_soft = nt_dot(grad, v_ref[:reach, lanes])
+            inner = jnp.sum(soft * grad_soft, 1, keepdims=True)
+            grad_logits = (soft * (grad_soft - inner)).astype(jnp.bfloat16)
+            dv_sum[:reach, :] += tn_dot(soft.astype(jnp.bfloat16), grad)
+            dk_sum[:reach, :] += tn_dot(grad_logits, query)
+            dq = dq + jnp.dot(
+                grad_logits, only(keys, head), preferred_element_type=jnp.float32
+            )
+            wide = grad_logits.astype(jnp.float32)
+            for j in range(block + 1):
+                skew_ref[head, block - j] += wide[:, j * LANES : (j + 1) * LANES]
+        dq_ref[rows, lanes] = (dq * scale).astype(jnp.bfloat16)
+    dk_ref[:, lanes] = (dk_sum[...] * scale).astype(jnp.bfloat16)
+    dv_ref[:, lanes] = dv_sum[...].astype(jnp.bfloat16)
+    for head in range(2):
+        for offset in range(blocks):
+            flipped = jnp.dot(
+                upside,
+                skew_ref[head, offset],
+                precision=HIGH,
+                preferred_element_type=jnp.float32,
+            )
+            padded = jnp.concatenate([flipped, jnp.zeros_like(flipped)], 1)
+            lined = pltpu.roll(padded, 0, 1, stride=1, stride_axis=0)
+            diag_ref[pair, head, offset, :] = jnp.sum(lined, 0)
+
+
+def finish_math(
+    x_ref,
+    query_ref,
+    key_ref,
+    value_ref,
+    gain_ref,
+    dq_ref,
+    dk_ref,
+    dv_ref,
+    grad_residual_ref,
+    gain_grad_ref,
+    input_grad_ref,
+):
+    grad_normed = nt_dot(dq_ref[...], query_ref[...])
+    grad_normed = grad_normed + nt_dot(dk_ref[...], key_ref[...])
+    grad_normed = grad_normed + nt_dot(dv_ref[...], value_ref[...])
+    inputs = x_ref[...].astype(jnp.float32)
+    from_norm, grad_gain = norm_back(inputs, gain_ref[0:1, :], grad_normed)
+    gain_grad_ref[0:1, :] = grad_gain
+    input_grad_ref[...] = (grad_residual_ref[...] + from_norm).astype(jnp.bfloat16)
+
+
+def backward_kernel(
+    experts,
+    capacity,
+    length_ref,
     x_ref,
     g_ref,
     routes_ref,
@@ -284,121 +447,59 @@
     diag_ref,
     grad_mix_ref,
     grad_residual_ref,
-    table_ref,
-    dk_sum,
-    dv_sum,
-    skew_ref,
+    *scratch,
 ):
-    tokens, width = x_ref.shape
-    blocks = tokens // LANES
-    scale = (LANES // 2) ** (-0.5)
-    grad_result = g_ref[...].astype(jnp.float32)
-    residual = residual_ref[...]
-    places, picks = column_places(routes_ref, experts, capacity)
-    gates = [gates_ref[:, pick : pick + 1] for pick in range(2)]
-    slots = out_rows_ref.shape[1]
-    picked = [jnp.zeros((tokens, width), jnp.float32) for _ in range(2)]
-    grad_normed = jnp.zeros((tokens, width), jnp.float32)
-    for index in range(0, out_rows_ref.shape[0], 2):
-        slot = (column_iota(tokens, 2 * slots) + index * slots).astype(jnp.float32)
-        hot = [jnp.where(slot == place, 1.0, 0.0) for place in places]
-        out_rows = out_rows_ref[index : index + 2].reshape(2 * slots, width)
-        back_rows = back_rows_ref[index : index + 2].reshape(2 * slots, width)
-        for pick in range(2):
-            picked[pick] = picked[pick] + jnp.dot(
-                hot[pick].astype(jnp.bfloat16), out_rows, preferred_element_type=jnp.float32
-            )
-        grad_normed = grad_normed + jnp.dot(
-            (hot[0] + hot[1]).astype(jnp.bfloat16), back_rows, preferred_element_type=jnp.float32
-        )
-    result_ref[...] = (residual + (gates[0] * picked[0] + gates[1] * picked[1])).astype(
-        jnp.bfloat16
+    combine_math(
+        experts,
+        capacity,
+        g_ref,
+        routes_ref,
+        output_ref,
+        router_ref,
+        gain_ref,
+        residual_ref,
+        gates_ref,
+        out_rows_ref,
+        back_rows_ref,
+        result_ref,
+        branch_ref,
+        router_grad_ref,
+        gain_grad_ref,
+        grad_mix_ref,
+        grad_residual_ref,
     )
-    grad_gates = [jnp.sum(grad_result * rows, 1, keepdims=True) for rows in picked]
-    common = gates[0] * grad_gates[0] + gates[1] * grad_gates[1]
-    grad_router = jnp.zeros((tokens, LANES), jnp.float32)
-    for pick in range(2):
-        grad_router = grad_router + jnp.where(
-            picks[pick], gates[pick] * (grad_gates[pick] - common), 0.0
-        )
-    normed = (residual * unit(residual) * gain_ref[1:2, :]).astype(jnp.bfloat16)
-    router_grad = jnp.zeros((width, LANES), jnp.float32)
-    for part in split(grad_router):
-        grad_normed = grad_normed + nt_dot(part, router_ref[...])
-        router_grad = router_grad + tn_dot(normed, part)
-    router_grad_ref[...] = router_grad
-    from_norm, grad_gain = norm_back(residual, gain_ref[1:2, :], grad_normed)
-    gain_grad_ref[1:2, :] = grad_gain
-    grad_residual = grad_result + from_norm
-    grad_residual_ref[...] = grad_residual
-    branch = grad_residual.astype(jnp.bfloat16)
-    branch_ref[...] = branch
-    grad_mix_ref[...] = nt_dot(branch, output_ref[...]).astype(jnp.bfloat16)
-    tick()
-
-    row, column = row_iota(LANES, LANES), column_iota(LANES, LANES)
-    upside = (row + column == LANES - 1).astype(jnp.float32)
 
     def attend_back(pair, carry):
-        lanes = pl.ds(pl.multiple_of(pair * LANES, LANES), LANES)
-        fill_bias(bias_ref.at[pl.ds(pair, 1)], table_ref, blocks)
-        dk_sum[...] = jnp.zeros_like(dk_sum)
-        dv_sum[...] = jnp.zeros_like(dv_sum)
-        skew_ref[...] = jnp.zeros_like(skew_ref)
-        for block in range(blocks):
-            rows = pl.ds(block * LANES, LANES)
-            reach = (block + 1) * LANES
-            dq = jnp.zeros((LANES, LANES), jnp.float32)
-            for head in range(2):
-                query = only(q_ref[rows, lanes], head)
-                grad = only(grad_mix_ref[rows, lanes], head)
-                keys = k_ref[:reach, lanes]
-                logits = masked_logits(query, keys, table_ref, head, block, length)
-                exponent = jnp.exp(logits - jnp.max(logits, 1, keepdims=True))
-                soft = exponent / jnp.sum(exponent, 1, keepdims=True)
-                grad_soft = nt_dot(grad, v_ref[:reach, lanes])
-                inner = jnp.sum(soft * grad_soft, 1, keepdims=True)
-                grad_logits = (soft * (grad_soft - inner)).astype(jnp.bfloat16)
-                dv_sum[:reach, :] += tn_dot(soft.astype(jnp.bfloat16), grad)
-                dk_sum[:reach, :] += tn_dot(grad_logits, query)
-                dq = dq + jnp.dot(
-                    grad_logits, only(keys, head), preferred_element_type=jnp.float32
-                )
-                wide = grad_logits.astype(jnp.float32)
-                for j in range(block + 1):
-                    skew_ref[head, block - j] += wide[:, j * LANES : (j + 1) * LANES]
-            dq_ref[rows, lanes] = (dq * scale).astype(jnp.bfloat16)
-        dk_ref[:, lanes] = (dk_sum[...] * scale).astype(jnp.bfloat16)
-        dv_ref[:, lanes] = dv_sum[...].astype(jnp.bfloat16)
-        for head in range(2):
-            for offset in range(blocks):
-                flipped = jnp.dot(
-                    upside,
-                    skew_ref[head, offset],
-                    precision=HIGH,
-                    preferred_element_type=jnp.float32,
-                )
-                padded = jnp.concatenate([flipped, jnp.zeros_like(flipped)], 1)
-                lined = pltpu.roll(padded, 0, 1, stride=1, stride_axis=0)
-                diag_ref[pair, head, offset, :] = jnp.sum(lined, 0)
+        attend_back_math(
+            pair,
+            length_ref[0],
+            q_ref,
+            k_ref,
+            v_ref,
+            grad_mix_ref,
+            bias_ref,
+            dq_ref,
+            dk_ref,
+            dv_ref,
+            diag_ref,
+            *scratch,
+        )
         return carry
 
-    pairs = width // LANES
-    lax.fori_loop(0, pairs // 2, attend_back, 0)
-    tick()
-    lax.fori_loop(pairs // 2, pairs, attend_back, 0)
-    tick()
-    grad_normed = nt_dot(dq_ref[...], query_ref[...])
-    grad_normed = grad_normed + nt_dot(dk_ref[...], key_ref[...])
-    grad_normed = grad_normed + nt_dot(dv_ref[...], value_ref[...])
-    inputs = x_ref[...].astype(jnp.float32)
-    from_norm, grad_gain = norm_back(inputs, gain_ref[0:1, :], grad_normed)
-    gain_grad_ref[0:1, :] = grad_gain
-    input_grad_ref[...] = (grad_residual_ref[...] + from_norm).astype(jnp.bfloat16)
-
-
-def backward_kernel(experts, capacity, length_ref, *refs):
-    backward_math(experts, capacity, lambda: None, length_ref[0], *refs)
+    lax.fori_loop(0, x_ref.shape[1] // LANES, attend_back, 0)
+    finish_math(
+        x_ref,
+        query_ref,
+        key_ref,
+        value_ref,
+        gain_ref,
+        dq_ref,
+        dk_ref,
+        dv_ref,
+        grad_residual_ref,
+        gain_grad_ref,
+        input_grad_ref,
+    )
 
 
 VMEM = pl.BlockSpec(memory_space=pltpu.VMEM)
@@ -425,7 +526,10 @@
         ),
         in_specs=[SMEM, rows, rows, *([VMEM] * 9)],
         out_specs=[VMEM] * 8,
-        scratch_shapes=[pltpu.VMEM((2, blocks, LANES, LANES), jnp.float32)],
+        scratch_shapes=[
+            pltpu.VMEM((tokens, width), jnp.bfloat16),
+            pltpu.VMEM((2, blocks, LANES, LANES), jnp.float32),
+        ],
         compiler_params=pltpu.CompilerParams(vmem_limit_bytes=56 * 2**20),
         cost_estimate=pl.CostEstimate(
             flops=2 * tokens * width * (4 * width + 4 * tokens + 6 * tokens),
@@ -600,7 +704,8 @@
     return list(inner), list(outer.reshape(count, size, width))
 
 
-FOLD_ORDERS = (("y", "x", "zl", "zh"), ("x", "zl", "y", "zh"), ("zl", "y", "x", "zh"))
+FOLD_ORDERS = (("x", "y", "zl", "zh"), ("y", "x", "zl", "zh"))
+FOLD_STEPS = 9
 
 
 def greet(axes):
@@ -628,12 +733,12 @@
     return copy
 
 
-def fold_math(operands, ready_ref, outs, grads, sums, inboxes, send_sem, recv_sem):
+def folder(operands, outs, grads, sums, inboxes, send_sem, recv_sem):
     count = len(outs)
-    grads = [*grads, ready_ref]
     mine = {axis: lax.axis_index(axis) for axis in ("core", "y", "x", "zl", "zh")}
     core = mine["core"]
     orders = [FOLD_ORDERS[i % len(FOLD_ORDERS)] for i in range(count)]
+    spread, joined = ("y", "x", "zl"), ("x", "zl")
 
     def cut(ref, i, depth, axes, partner=None):
         done = orders[i][:depth]
@@ -647,70 +752,55 @@
             columns = pl.ds(pl.multiple_of(place["zh"] * width, LANES), width)
         return ref.at[(*index, slice(None), columns)]
 
-    spread, joined = ("y", "x", "zl"), ("x", "zl")
-    started = []
-    flying = []
-    for i in range(count):
-        if i < count - 1:
-            left_0, right_0, left_1, right_1 = operands[i]
-            total = tn_dot(left_0[...], right_0[...]) + tn_dot(left_1[...], right_1[...])
-            grads[i][...] = total.astype(jnp.bfloat16).reshape(grads[i].shape)
-        flying.append(
-            push(
-                grads[i].at[:, 1 - core],
-                inboxes[0][i],
-                send_sem.at[i, 0],
-                recv_sem.at[i, 0],
-                "core",
-            )
-        )
-    for step in range(5):
+    def copy(i, k):
+        if k == 0:
+            source, target, axis = grads[i].at[:, 1 - core], inboxes[0][i], "core"
+        elif k < 5:
+            axis = orders[i][k - 1]
+            source, target = cut(sums[i], i, k, spread, axis), inboxes[k][i]
+        else:
+            axis = [axis for axis in reversed(orders[i]) if axis != "y"][k - 5]
+            source = target = cut(outs[i], i, orders[i].index(axis) + 1, joined)
+        return pltpu.make_async_remote_copy(
+            src_ref=source,
+            dst_ref=target,
+            send_sem=send_sem.at[i, k],
+            recv_sem=recv_sem.at[i, k],
+            device_id={axis: 1 - mine[axis]},
+            device_id_type=pl.DeviceIdType.MESH,
+        )
+
+    def step(i, k):
+        if k == 0:
+            if operands[i] is not None:
+                left_0, right_0, left_1, right_1 = operands[i]
+                total = tn_dot(left_0[...], right_0[...]) + tn_dot(left_1[...], right_1[...])
+                grads[i][...] = total.astype(jnp.bfloat16).reshape(grads[i].shape)
+            copy(i, 0).start()
+            return
+        copy(i, k - 1).wait_recv()
+        if k == 1:
+            total = grads[i][:, core].astype(jnp.float32) + inboxes[0][i][...].astype(jnp.float32)
+            sums[i][...] = total.astype(jnp.bfloat16)
+        elif k < 6:
+            kept = cut(sums[i], i, k - 1, spread)
+            total = kept[...].astype(jnp.float32) + inboxes[k - 1][i][...].astype(jnp.float32)
+            target = kept if k < 5 else cut(outs[i], i, 4, joined)
+            target[...] = total.astype(jnp.bfloat16)
+        if k < FOLD_STEPS - 1:
+            copy(i, k).start()
+
+    def finish():
         for i in range(count):
-            flying[i].wait_recv()
-            if step == 0:
-                sums[i][...] = (
-                    grads[i][:, core].astype(jnp.float32)
-                    + inboxes[0][i][...].astype(jnp.float32)
-                ).astype(jnp.bfloat16)
-            else:
-                kept = cut(sums[i], i, step, spread)
-                total = kept[...].astype(jnp.float32) + inboxes[step][i][...].astype(jnp.float32)
-                kept[...] = total.astype(jnp.bfloat16)
-            started.append(flying[i])
-            if step < 4:
-                axis = orders[i][step]
-                flying[i] = push(
-                    cut(sums[i], i, step + 1, spread, axis),
-                    inboxes[step + 1][i],
-                    send_sem.at[i, step + 1],
-                    recv_sem.at[i, step + 1],
-                    axis,
-                )
-    for i in range(count):
-        cut(outs[i], i, 4, joined)[...] = cut(sums[i], i, 4, spread)[...]
-    left = [[axis for axis in reversed(order)] for order in orders]
-    for step in range(4):
-        for i in range(count):
-            if step:
-                if flying[i] is not None:
-                    flying[i].wait_recv()
-                    started.append(flying[i])
-            axis = left[i][step]
-            flying[i] = None
-            if axis != "y":
-                place = cut(outs[i], i, 4 - step, joined)
-                flying[i] = push(
-                    place, place, send_sem.at[i, 5 + step], recv_sem.at[i, 5 + step], axis
-                )
-    for i in range(count):
-        if flying[i] is not None:
-            flying[i].wait_recv()
-            started.append(flying[i])
-    for copy in started:
-        copy.wait_send()
+            for k in range(FOLD_STEPS - 1):
+                copy(i, k).wait_send()
+
+    return step, finish
 
 
 PEER_AXES = ("y", "zl", "x")
+PEER_BITS = {"x": 1, "zl": 2, "y": 4}
+DENSE_AXES = ("zl", "y")
 CHUNKS = 4
 
 
@@ -770,9 +860,10 @@
     arrived_ref, refs = refs[0], refs[1:]
     normed_ref, q_ref, k_ref, v_ref, mix_ref, residual_ref, gates_ref, gain_ref, bias_ref = refs[:9]
     refs = refs[9:]
-    sent_refs, relays = refs[:2], refs[2:4]
-    table_ref = refs[4]
-    mixer_send, mixer_recv, move_send, move_recv, row_send, row_recv, local_sem = refs[5:]
+    sent_refs, token_refs, token_boxes, g_boxes, gate_boxes, route_boxes = refs[:6]
+    relays, table_ref, refs = refs[6:8], refs[8], refs[9:]
+    mixer_send, mixer_recv, move_send, move_recv, row_send, row_recv, local_sem = refs[:7]
+    share_send, share_recv = refs[7:]
     core, y, x, zh = (lax.axis_index(axis) for axis in ("core", "y", "x", "zh"))
     at_home = zh == y
     away = zh != y
@@ -854,6 +945,13 @@
             start = start + half_at * size
         return whole.at[pl.ds(pl.multiple_of(start, size), size)]
 
+    shared = {}
+
+    def share(b, kind, source, box):
+        shared[b, kind] = send(
+            source, box, share_send.at[b, kind], share_recv.at[b, kind], across(DENSE_AXES[b])
+        )
+
     mixers = []
     for i, (part, whole) in enumerate(zip(parts, wholes)):
         for j, axis in enumerate(("y", "core")):
@@ -862,6 +960,9 @@
             mixers.append(push(source, place, mixer_send.at[i, j], mixer_recv.at[i, j], axis))
     for chunk in range(CHUNKS):
         move_z(0, chunk)
+    for b in range(batch):
+        share(b, 0, g_ref.at[b], g_boxes.at[b])
+        share(b, 1, routes_t_ref.at[b], route_boxes.at[b])
     for i, (part, whole) in enumerate(zip(parts, wholes)):
         spot(part, whole, y, core)[...] = part[...]
     for i, whole in enumerate(wholes):
@@ -873,9 +974,8 @@
         mixers[2 * count + 2 * i].wait_recv()
         place = spot(parts[i], whole, 1 - y, core, 1 - x)
         mixers.append(push(place, place, mixer_send.at[i, 4], mixer_recv.at[i, 4], "core"))
-    for which in range(2):
-        for chunk in range(CHUNKS):
-            move_first(which, chunk)
+    for chunk in range(CHUNKS):
+        move_first(0, chunk)
 
     @pl.when(at_home)
     def _():
@@ -899,20 +999,17 @@
                 row : row + 1, offset * 2 * LANES : (offset + 1) * 2 * LANES
             ]
 
-    rows_flying = []
-    for b in range(batch):
+    flying = []
+
+    def forward(b):
         forward_math(
-            experts,
-            capacity,
             lengths_ref[b],
             x_ref.at[b],
-            g_ref.at[b],
             routes_ref.at[b],
-            routes_t_ref.at[b],
             *wholes[:5],
             gain_ref,
             bias_ref,
-            sent_refs[b],
+            token_refs.at[b],
             normed_ref.at[b],
             q_ref.at[b],
             k_ref.at[b],
@@ -922,27 +1019,66 @@
             gates_ref.at[b],
             table_ref,
         )
-        _, mine = peer_of(0)
-        local = pltpu.make_async_copy(
-            sent_refs[b].at[mine], arrived_ref.at[b, mine], local_sem.at[2 + b]
-        )
-        local.start()
-        rows_flying.append(local)
-        for turn, step in enumerate((7, 1, 6, 2, 5, 3, 4)):
+        share(b, 2, token_refs.at[b], token_boxes.at[b])
+        share(b, 3, gates_ref.at[b], gate_boxes.at[b])
+
+    def dispatch(b, relayed):
+        axis = DENSE_AXES[b]
+        bit = PEER_BITS[axis]
+        if relayed:
+            for kind in range(4):
+                shared[b, kind].wait_recv()
+            fill = dispatcher(
+                experts,
+                capacity,
+                token_boxes.at[b],
+                g_boxes.at[b],
+                gate_boxes.at[b],
+                route_boxes.at[b],
+            )
+        else:
+            fill = dispatcher(
+                experts,
+                capacity,
+                token_refs.at[b],
+                g_ref.at[b],
+                gates_ref.at[b],
+                routes_t_ref.at[b],
+            )
+        _, source = peer_of(bit if relayed else 0)
+        steps = [step for step in (7, 5, 6, 3, 4, 1, 2, 0) if not step & bit]
+        for turn, step in enumerate(steps):
             target, block = peer_of(step)
-            copy = send(
-                sent_refs[b].at[block],
-                arrived_ref.at[b, mine],
-                row_send.at[b, step - 1],
-                row_recv.at[b, step - 1],
-                target,
-            )
-            rows_flying.append(copy)
-            if b == 0 and turn % 2 == 0:
-                move_z(1, turn // 2)
-        if b == 0:
-            for chunk in range(CHUNKS):
-                relay_z(0, chunk)
+            place = sent_refs.at[b, 4 * relayed + turn]
+            fill(block, place)
+            if step:
+                copy = send(
+                    place,
+                    arrived_ref.at[b, source],
+                    row_send.at[b, 4 * relayed + turn],
+                    row_recv.at[b, source],
+                    target,
+                )
+                flying.append(copy)
+            else:
+                copy = pltpu.make_async_copy(
+                    place, arrived_ref.at[b, source], local_sem.at[2 + 2 * b + relayed]
+                )
+                copy.start()
+                flying.append(copy)
+
+    forward(0)
+    for chunk in range(CHUNKS):
+        move_z(1, chunk)
+    dispatch(0, 0)
+    forward(1)
+    for chunk in range(CHUNKS):
+        relay_z(0, chunk)
+    dispatch(0, 1)
+    dispatch(1, 0)
+    for chunk in range(CHUNKS):
+        move_first(1, chunk)
+    dispatch(1, 1)
     for chunk in range(CHUNKS):
         relay_y(0, chunk)
     for chunk in range(CHUNKS):
@@ -960,8 +1096,26 @@
 
     for copy in mixers:
         copy.wait_send()
-    for copy in rows_flying:
-        copy.wait()
+    for copy in flying:
+        if copy.is_remote:
+            copy.wait_send()
+        else:
+            copy.wait()
+    for b in range(batch):
+        for kind in range(4):
+            shared[b, kind].wait_send()
+        bit = PEER_BITS[DENSE_AXES[b]]
+        for step in range(8):
+            if step & ~bit:
+                target, block = peer_of(step)
+                pltpu.make_async_remote_copy(
+                    src_ref=sent_refs.at[b, 0],
+                    dst_ref=arrived_ref.at[b, block],
+                    send_sem=row_send.at[b, 0],
+                    recv_sem=row_recv.at[b, block],
+                    device_id=target,
+                    device_id_type=pl.DeviceIdType.MESH,
+                ).wait_recv()
 
 
 def layer_head(experts, capacity, lengths, x, g, routes, routes_t, inner, outer, parts, bias_shape):
@@ -990,8 +1144,10 @@
         in_specs=[SMEM, *([VMEM] * (6 + count))],
         out_specs=[*([VMEM] * count), *([anywhere] * 9), *([VMEM] * 9)],
         scratch_shapes=[
-            pltpu.VMEM(exchange, jnp.bfloat16),
-            pltpu.VMEM(exchange, jnp.bfloat16),
+            pltpu.VMEM((batch, *exchange), jnp.bfloat16),
+            *([pltpu.VMEM(x.shape, jnp.bfloat16)] * 3),
+            pltpu.VMEM((batch, tokens, LANES), jnp.float32),
+            pltpu.VMEM(routes_t.shape, jnp.int32),
             pltpu.VMEM(inner.shape, jnp.bfloat16),
             pltpu.VMEM(outer.shape, jnp.bfloat16),
             pltpu.VMEM((2, blocks, LANES, LANES), jnp.float32),
@@ -999,9 +1155,11 @@
             dma((count, 5)),
             dma((2, CHUNKS, 4)),
             dma((2, CHUNKS, 4)),
-            dma((batch, 7)),
-            dma((batch, 7)),
-            dma((4,)),
+            dma((batch, 8)),
+            dma((batch, 8)),
+            dma((6,)),
+            dma((batch, 4)),
+            dma((batch, 4)),
         ],
         compiler_params=pltpu.CompilerParams(
             collective_id=1, has_side_effects=True, vmem_limit_bytes=60 * 2**20
@@ -1212,21 +1370,32 @@
     return jnp.sum(jnp.where(row_iota(sums.shape[0], width) == head, sums, 0.0), 0, keepdims=True)
 
 
+FOLD_SPLIT = 4
+
+
 def tail_kernel(experts, capacity, bucket_count, lengths_ref, *refs):
     x_ref, g_ref, routes_ref, refs = refs[0], refs[1], refs[2], refs[3:]
     weights, gain_ref, bias_ref, refs = refs[:5], refs[5], refs[6], refs[7:]
     normed_ref, q_ref, k_ref, v_ref, mix_ref, residual_ref, gates_ref, returned_ref = refs[:8]
     partials, refs = refs[8:12], refs[12:]
-    result_ref, input_grad_ref, home_refs, outs, refs = refs[0], refs[1], refs[2:4], refs[4:9], refs[9:]
+    result_ref, input_grad_ref, home_refs, outs, refs = (
+        refs[0],
+        refs[1],
+        refs[2:4],
+        refs[4:12],
+        refs[12:],
+    )
     out_rows, back_rows, branch, dq, dk, dv, router_grad, gain_grad, diag, refs = *refs[:9], refs[9:]
-    scratch, ready, grads, sums, refs = refs[:6], refs[6], refs[7:11], refs[11:16], refs[16:]
-    inboxes, refs = [refs[5 * i : 5 * i + 5] for i in range(5)], refs[25:]
+    grad_mix, grad_residual, scratch, refs = refs[0], refs[1], refs[2:6], refs[6:]
+    grads, sums, refs = refs[:8], refs[8:16], refs[16:]
+    inboxes, refs = [refs[8 * i : 8 * i + 8] for i in range(5)], refs[40:]
     fetched, landed, fold_send, fold_recv, move_send, move_recv, local_sem, own_sem = refs
     y, zh = lax.axis_index("y"), lax.axis_index("zh")
     at_home, away = zh == y, zh != y
     batch, tokens, width = x_ref.shape
     far, near = partials[:2], partials[2:]
     rows = far[0].shape[0] // CHUNKS
+    cut_at = FOLD_SPLIT * LANES
 
     greet(("core", "y", "x", "zl", "zh"))
 
@@ -1256,89 +1425,144 @@
             device_id_type=pl.DeviceIdType.MESH,
         )
 
+    def move(index):
+        which, chunk = index // CHUNKS, index % CHUNKS
+        copy(which, chunk, 0, far[which], fetched.at[which], "y").wait_recv()
+
+        @pl.when(at_home)
+        def _():
+            copy(which, chunk, 1, fetched.at[which], landed.at[which], "zh").start()
+
+        @pl.when(away)
+        def _():
+            copy(which, chunk, 1, near[which], landed.at[which], "zh").start()
+
     order = [(which, chunk) for which in range(2) for chunk in range(CHUNKS)]
     for which, chunk in order:
         copy(which, chunk, 0, far[which], fetched.at[which], "y").start()
-
-        @pl.when(away)
-        def _():
-            copy(which, chunk, 1, near[which], landed.at[which], "zh").start()
-
-    waiting = list(order)
-
-    def tick(amount=2):
-        for which, chunk in waiting[:amount]:
-            copy(which, chunk, 0, far[which], fetched.at[which], "y").wait_recv()
-
-            @pl.when(at_home)
-            def _():
-                copy(which, chunk, 1, fetched.at[which], landed.at[which], "zh").start()
-
-        del waiting[:amount]
-
     for part in load(0):
         part.start()
+
+    def columns(ref, b, first):
+        return ref.at[b, :, :cut_at] if first else ref.at[b, :, cut_at:]
+
+    operands = [(mix_ref.at[0], branch.at[0], mix_ref.at[1], branch.at[1])]
+    for first in (True, False):
+        for ref in (dq, dk, dv):
+            operands.append(
+                (
+                    normed_ref.at[0],
+                    columns(ref, 0, first),
+                    normed_ref.at[1],
+                    columns(ref, 1, first),
+                )
+            )
+    operands.append(None)
+    fold, fold_end = folder(operands, outs, grads, sums, inboxes, fold_send, fold_recv)
+    early, late, small = (1, 2, 3), (4, 5, 6), 7
+
     for b in range(batch):
         for part in load(b):
             part.wait()
-
-        def combined():
-            if b + 1 < batch:
-                for part in load(b + 1):
-                    part.start()
-            else:
-                for which, chunk in order:
-                    own(which, chunk).start()
-            tick(1)
-
-        backward_math(
+        combine_math(
             experts,
             capacity,
-            Ticks([combined, tick, tick]),
-            lengths_ref[b],
-            x_ref.at[b],
             g_ref.at[b],
             routes_ref.at[b],
-            *weights,
+            weights[3],
+            weights[4],
             gain_ref,
-            bias_ref,
-            q_ref.at[b],
-            k_ref.at[b],
-            v_ref.at[b],
             residual_ref.at[b],
             gates_ref.at[b],
             out_rows,
             back_rows,
             result_ref.at[b],
-            input_grad_ref.at[b],
             branch.at[b],
+            router_grad.at[b],
+            gain_grad.at[b],
+            grad_mix.at[b],
+            grad_residual.at[b],
+        )
+        if b + 1 < batch:
+            for part in load(b + 1):
+                part.start()
+            move(0)
+        else:
+            for which, chunk in order:
+                own(which, chunk).start()
+            move(1)
+    fold(0, 0)
+
+    actions = {
+        0: [(fold, 0, 1), (move, 2)],
+        3: [(fold, 0, 2), (move, 3)],
+        5: [(move, 4)],
+        7: [*((fold, i, 0) for i in early), (move, 5)],
+        9: [*((fold, i, 1) for i in early), (fold, 0, 3)],
+        10: [(move, 6)],
+        11: [*((fold, i, 2) for i in early), (move, 7)],
+    }
+
+    def act(moment):
+        for action, *values in actions[moment]:
+            action(*values)
+
+    def attend_back(item, carry):
+        pair, b = item // 2, lax.rem(item, 2)
+        attend_back_math(
+            pair,
+            lengths_ref[b],
+            q_ref.at[b],
+            k_ref.at[b],
+            v_ref.at[b],
+            grad_mix.at[b],
+            bias_ref,
             dq.at[b],
             dk.at[b],
             dv.at[b],
-            router_grad.at[b],
-            gain_grad.at[b],
             diag.at[b],
             *scratch,
         )
-    tick(len(order))
-
+        for moment in actions:
+            pl.when(item == moment)(functools.partial(act, moment))
+        return carry
+
+    lax.fori_loop(0, batch * (width // LANES), attend_back, 0)
+    for i in late:
+        fold(i, 0)
+    for i in early:
+        fold(i, 3)
+
+    def finish(b):
+        finish_math(
+            x_ref.at[b],
+            *weights[:3],
+            gain_ref,
+            dq.at[b],
+            dk.at[b],
+            dv.at[b],
+            grad_residual.at[b],
+            gain_grad.at[b],
+            input_grad_ref.at[b],
+        )
+
+    finish(0)
+    for i in late:
+        fold(i, 1)
+    fold(0, 4)
+    finish(1)
     lines = [
         jnp.concatenate(
             [
-                jnp.concatenate(
-                    [
-                        diag[0, head // 2, head % 2, offset : offset + 1, :]
-                        + diag[1, head // 2, head % 2, offset : offset + 1, :]
-                        for offset in range(diag.shape[3])
-                    ],
-                    1,
-                )
-                for head in range(2 * diag.shape[1])
+                diag[0, head // 2, head % 2, offset : offset + 1, :]
+                + diag[1, head // 2, head % 2, offset : offset + 1, :]
+                for offset in range(diag.shape[3])
             ],
-            0,
-        )
+            1,
+        )
+        for head in range(2 * diag.shape[1])
     ]
-    lines.append(jnp.zeros((16 - lines[0].shape[0], lines[0].shape[1]), jnp.float32))
+    lines.append(jnp.zeros((16 - len(lines), width), jnp.float32))
     bias_line = bias_columns(jnp.concatenate(lines, 0), 4, bucket_count)
     gain_lines = gain_grad[0] + gain_grad[1]
     row = row_iota(LANES, width)
@@ -1348,22 +1572,15 @@
         jnp.where(row == 1, gain_lines[1:2, :], jnp.where(row == 2, bias_line, 0.0)),
     )
     packed = jnp.concatenate([router_grad[0] + router_grad[1], stacked.T], 1)
-    ready[...] = packed.astype(jnp.bfloat16).reshape(ready.shape)
-    fold_math(
-        [
-            (normed_ref.at[0], dq.at[0], normed_ref.at[1], dq.at[1]),
-            (normed_ref.at[0], dk.at[0], normed_ref.at[1], dk.at[1]),
-            (normed_ref.at[0], dv.at[0], normed_ref.at[1], dv.at[1]),
-            (mix_ref.at[0], branch.at[0], mix_ref.at[1], branch.at[1]),
-        ],
-        ready,
-        outs,
-        grads,
-        sums,
-        inboxes,
-        fold_send,
-        fold_recv,
-    )
+    grads[small][...] = packed.astype(jnp.bfloat16).reshape(grads[small].shape)
+    fold(small, 0)
+    reached = {0: 5, small: 1, **dict.fromkeys(early, 4), **dict.fromkeys(late, 2)}
+    while min(reached.values()) < FOLD_STEPS:
+        for i in (*late, small, *early, 0):
+            if reached[i] < FOLD_STEPS:
+                fold(i, reached[i])
+                reached[i] += 1
+    fold_end()
 
     for which, chunk in order:
         own(which, chunk).wait()
@@ -1377,14 +1594,6 @@
 
         pl.when(at_home)(lambda: settle((out_rows, back_rows)[which][chunk]))
         pl.when(away)(lambda: settle(fetched[which, place]))
-
-
-class Ticks:
-    def __init__(self, actions):
-        self.actions = list(actions)
-
-    def __call__(self):
-        self.actions.pop(0)()
 
 
 def layer_tail(experts, capacity, bucket_count, lengths, x, g, routes, weights, gains, bias, saved, returned, partials):
@@ -1394,7 +1603,9 @@
     anywhere = pl.BlockSpec(memory_space=pl.ANY)
     flat = shape(x.shape, jnp.bfloat16)
     quarter = partials[0].shape
-    sizes = [(width // 16, width)] * 4 + [(width // 16, 2 * LANES)]
+    cut_at = FOLD_SPLIT * LANES
+    widths = [width, *([cut_at] * 3), *([width - cut_at] * 3), 2 * LANES]
+    sizes = [(width // 16, columns) for columns in widths]
     boxes = []
     for depth in range(5):
         for i, (part, columns) in enumerate(sizes):
@@ -1415,7 +1626,7 @@
             *(shape((2, 2, *size), jnp.bfloat16) for size in sizes),
         ),
         in_specs=[SMEM, *([VMEM] * (3 + 5 + 2 + 7)), *([anywhere] * 5)],
-        out_specs=[VMEM] * 9,
+        out_specs=[VMEM] * 12,
         scratch_shapes=[
             pltpu.VMEM(side, jnp.bfloat16),
             pltpu.VMEM(side, jnp.bfloat16),
@@ -1423,20 +1634,19 @@
             pltpu.VMEM((batch, width, LANES), jnp.float32),
             pltpu.VMEM((batch, 2, width), jnp.float32),
             pltpu.VMEM((batch, *bias.shape), jnp.float32),
-            pltpu.VMEM((tokens, width), jnp.bfloat16),
-            pltpu.VMEM((tokens, width), jnp.float32),
+            pltpu.VMEM((batch, tokens, width), jnp.bfloat16),
+            pltpu.VMEM((batch, tokens, width), jnp.float32),
             pltpu.VMEM((2, blocks, LANES, LANES), jnp.float32),
             pltpu.VMEM((tokens, LANES), jnp.float32),
             pltpu.VMEM((tokens, LANES), jnp.float32),
             pltpu.VMEM((2, blocks, LANES, LANES), jnp.float32),
-            pltpu.VMEM((2, 2, 2, 2, *sizes[-1]), jnp.bfloat16),
-            *(pltpu.VMEM((2, 2, 2, 2, *size), jnp.bfloat16) for size in sizes[:-1]),
+            *(pltpu.VMEM((2, 2, 2, 2, *size), jnp.bfloat16) for size in sizes),
             *(pltpu.VMEM((2, 2, 2, *size), jnp.bfloat16) for size in sizes),
             *boxes,
             pltpu.VMEM((2, *quarter), jnp.bfloat16),
             pltpu.VMEM((2, *quarter), jnp.bfloat16),
-            dma((5, 9)),
-            dma((5, 9)),
+            dma((8, FOLD_STEPS - 1)),
+            dma((8, FOLD_STEPS - 1)),
             dma((2, CHUNKS, 2)),
             dma((2, CHUNKS, 2)),
             dma((2,)),
@@ -1447,7 +1657,11 @@
         ),
         name="layer_tail",
     )(lengths, x, g, routes, *weights, gains, bias, *saved, returned, *partials)
-    folded = [out.reshape(-1, out.shape[-1]).astype(jnp.float32) for out in results[4:]]
+    output, *rest, packed = (
+        out.reshape(-1, out.shape[-1]).astype(jnp.float32) for out in results[4:]
+    )
+    folded = [jnp.concatenate(pair, 1) for pair in zip(rest[:3], rest[3:])]
+    folded += [output, packed]
     homes = [home.astype(jnp.float32) for home in results[2:4]]
     return results[0], results[1], folded, homes
 
@@ -1669,7 +1883,7 @@
         tokens,
         cotangent,
         routes,
-        routes.swapaxes(1, 2),
+        jnp.pad(routes.swapaxes(1, 2), ((0, 0), (0, 6), (0, 0))),
         inner_weight[0],
         outer_weight[0],
         parts,

time: 529 us -> 480 us (0.907)
  Pallas kernels: 501 us -> 452 us
    pallas_call x1, Pallas kernels: 203 us -> 166 us  [layer_head(): pl.pallas_call(functools.partial(head_kernel, experts, capacity), out_sha...]
    pallas_call x1, Pallas kernels: 166 us -> 154 us  [layer_tail(): pl.pallas_call(functools.partial(tail_kernel, experts, capacity, bucket_c...]
where the time goes in v1:
time: 480 us; the launch traced here: 474 us
  Pallas kernels  452 us (94%)
  local copies, waits for them, and re-layouts  11.4 us (2%)
  other arithmetic  8.36 us (2%)
    pallas_call x1, Pallas kernels, layer_head(): pl.pallas_call(functools.partial(head_kernel, experts, capacity), out_sha...  166 us
    pallas_call x1, Pallas kernels, layer_tail(): pl.pallas_call(functools.partial(tail_kernel, experts, capacity, bucket_c...  154 us
    pallas_call x1, Pallas kernels, layer_middle(): pl.pallas_call(middle_kernel, out_shape=(jax.ShapeDtypeStruct(arrived.sha...  132 us

profile of v1, /device:TPU:0, one launch (start us, length us, event | category | flops | bytes accessed | tf_op | source)
XLA Modules:
  0.0 473.7 jit_solution(8909805115655474957)
XLA Ops:
  0.6 0.0 copy-start
  0.7 1.4 fusion.8.lengths_ref
  2.0 0.7 stack.9
  2.7 0.7 stack.10
  3.4 0.1 tile.10
  3.5 0.0 copy-done
  3.5 1.0 fusion
  4.6 1.3 pad.12.routes_t_ref
  5.9 0.6 fusion.3.refs_5_
  6.5 0.8 copy.40
  7.3 0.6 pad.13.refs_4_
  8.0 1.6 copy.42.routes_ref.refs_2_
  9.6 166.1 %layer_head.1 = (bf16[768,768]{1,0:T(8,128)(2,1)}, bf16[768,768]{1,0:T(8,128)(2,1)}, bf16[768,768]{1,0:T(8,128)(2,1)}, bf16[768,768]{1,0:T(8,128)(2,1)}, bf16[76...) custom-call(s32[2]{0:T(128)} %fusion.8.lengths_ref, ...), custom_call_target="tpu_custom_call" | custom-call | tf_op jit(solution)/shard_map/layer_head/pallas_call | solution.py:1132
  175.7 131.7 %layer_middle.1 = (bf16[2,8,2,192,768]{4,3,2,1,0:T(8,128)(2,1)}, bf16[768,768]{1,0:T(8,128)(2,1)}, bf16[768,768]{1,0:T(8,128)(2,1)}, bf16[768,768]{1,0:T(8,128)(2,1)}, bf16[768,768]{1,0:T(8,128)(2,1)}) custom-call(bf16[2,8,2,192,768]{4,3,2,1,0:T(8,128)(2,1)} %get-tuple-element.66.arrived_ref, bf16[768,768]{1,0:T(8,128)(2,1)} %get-tuple-element.67.refs_0_, ...), custom_call_target="tpu_custom_call" | custom-call | tf_op jit(solution)/shard_map/layer_middle/pallas_call | solution.py:1326
  307.3 153.8 %layer_tail.1 = (bf16[2,384,768]{2,1,0:T(8,128)(2,1)}, bf16[2,384,768]{2,1,0:T(8,128)(2,1)}, bf16[768,768]{1,0:T(8,128)(2,1)}, bf16[768,768]{1,0:T(8,128)(2,1)},...) custom-call(s32[2]{0:T(128)} %fusion.8.lengths_ref, ...), custom_call_target="tpu_custom_call" | custom-call | tf_op jit(solution)/shard_map/layer_tail/pallas_call | solution.py:1620
  461.2 0.0 copy-start.9
  461.2 1.0 bitcast_convert_fusion.3
  462.2 0.2 slice_reduce_fusion
  462.4 0.7 reshape_squeeze.3
  463.1 0.7 copy.47
  463.7 0.1 fusion.9
  463.8 0.6 copy.49
  464.5 0.6 copy.48
  465.1 0.0 copy-done.9
  465.1 0.9 maximum_convert_fusion.2
  466.0 0.9 bitcast_convert_fusion.2
  466.9 1.1 maximum_convert_fusion
  468.0 0.0 copy-done.3
  468.0 2.5 bitcast_convert_fusion
  470.5 1.0 copy.54
  471.5 0.7 copy-done.4
  472.2 1.0 copy.55
  (25 shorter events, 0.1 us)
Async XLA Ops:
  0.6 2.9 copy-start
  461.2 3.9 copy-start.9
  461.2 3.9 copy-start.12
  461.2 4.8 %copy-start.6 = (bf16[2,2,48,768]{3,2,1,0:T(8,128)(2,1)S(1)}, bf16[2,2,48,768]{3,2,1,0:T(8,128)(2,1)}, u32[]{:S(2)}) copy-start(bf16[2,2,48,768]{3,2,1,0:T(8,128)(2,1)} %get-tuple-element.88) | copy-start | bytes 884740
  463.7 3.1 copy-start.7
  463.7 3.1 copy-start.8
  463.7 3.1 copy-start.10
  463.7 3.1 copy-start.11
  466.0 2.0 copy-start.2
  466.0 2.0 copy-start.3
  468.0 2.5 copy-start.5
  470.5 1.7 copy-start.4
  470.5 2.7 copy-start.1

commit v2 on v1

--- a/solution.py
+++ b/solution.py
@@ -284,6 +284,7 @@
     gain_grad_ref,
     grad_mix_ref,
     grad_residual_ref,
+    tick=lambda: None,
 ):
     tokens, width = g_ref.shape
     grad_result = g_ref[...].astype(jnp.float32)
@@ -308,6 +309,7 @@
     result_ref[...] = (residual + (gates[0] * picked[0] + gates[1] * picked[1])).astype(
         jnp.bfloat16
     )
+    tick()
     grad_gates = [jnp.sum(grad_result * rows, 1, keepdims=True) for rows in picked]
     common = gates[0] * grad_gates[0] + gates[1] * grad_gates[1]
     grad_router = jnp.zeros((tokens, LANES), jnp.float32)
@@ -815,8 +817,8 @@
     return target, block
 
 
-def send(source, target, send_sem, recv_sem, device):
-    copy = pltpu.make_async_remote_copy(
+def send_later(source, target, send_sem, recv_sem, device):
+    return pltpu.make_async_remote_copy(
         src_ref=source,
         dst_ref=target,
         send_sem=send_sem,
@@ -824,6 +826,10 @@
         device_id=device,
         device_id_type=pl.DeviceIdType.MESH,
     )
+
+
+def send(*values):
+    copy = send_later(*values)
     copy.start()
     return copy
 
@@ -845,6 +851,7 @@
     experts,
     capacity,
     lengths_ref,
+    dealing_ref,
     x_ref,
     g_ref,
     routes_ref,
@@ -858,12 +865,13 @@
     wholes, refs = refs[:count], refs[count:]
     inner_outs, outer_outs, refs = refs[:4], refs[4:8], refs[8:]
     arrived_ref, refs = refs[0], refs[1:]
-    normed_ref, q_ref, k_ref, v_ref, mix_ref, residual_ref, gates_ref, gain_ref, bias_ref = refs[:9]
-    refs = refs[9:]
+    targets, gates_ref, gain_ref, bias_ref, refs = refs[:6], *refs[6:9], refs[9:]
     sent_refs, token_refs, token_boxes, g_boxes, gate_boxes, route_boxes = refs[:6]
     relays, table_ref, refs = refs[6:8], refs[8], refs[9:]
     mixer_send, mixer_recv, move_send, move_recv, row_send, row_recv, local_sem = refs[:7]
-    share_send, share_recv = refs[7:]
+    share_send, share_recv, keep_sem, *kept = refs[7:]
+    normed_ref, q_ref, k_ref, v_ref, mix_ref, residual_ref = kept[:6]
+    whole_targets, wholes = wholes[:5], [*kept[6:], wholes[5]]
     core, y, x, zh = (lax.axis_index(axis) for axis in ("core", "y", "x", "zh"))
     at_home = zh == y
     away = zh != y
@@ -945,11 +953,15 @@
             start = start + half_at * size
         return whole.at[pl.ds(pl.multiple_of(start, size), size)]
 
-    shared = {}
-
-    def share(b, kind, source, box):
-        shared[b, kind] = send(
-            source, box, share_send.at[b, kind], share_recv.at[b, kind], across(DENSE_AXES[b])
+    def share(b, kind):
+        source = (g_ref, routes_t_ref, token_refs, gates_ref)[kind]
+        box = (g_boxes, route_boxes, token_boxes, gate_boxes)[kind]
+        return send_later(
+            source.at[b],
+            box.at[b],
+            share_send.at[b, kind],
+            share_recv.at[b, kind],
+            across(DENSE_AXES[b]),
         )
 
     mixers = []
@@ -961,8 +973,8 @@
     for chunk in range(CHUNKS):
         move_z(0, chunk)
     for b in range(batch):
-        share(b, 0, g_ref.at[b], g_boxes.at[b])
-        share(b, 1, routes_t_ref.at[b], route_boxes.at[b])
+        share(b, 0).start()
+        share(b, 1).start()
     for i, (part, whole) in enumerate(zip(parts, wholes)):
         spot(part, whole, y, core)[...] = part[...]
     for i, whole in enumerate(wholes):
@@ -999,11 +1011,22 @@
                 row : row + 1, offset * 2 * LANES : (offset + 1) * 2 * LANES
             ]
 
-    flying = []
-
-    def forward(b):
+    keeps = [
+        pltpu.make_async_copy(source, target, keep_sem.at[index])
+        for index, (source, target) in enumerate(zip(wholes, whole_targets))
+    ]
+    for part in keeps:
+        part.start()
+
+    def keep(b):
+        return [
+            pltpu.make_async_copy(source.at[b], target.at[b], keep_sem.at[5 + 6 * b + index])
+            for index, (source, target) in enumerate(zip(kept, targets))
+        ]
+
+    def forward(b, carry):
         forward_math(
-            lengths_ref[b],
+            lengths_ref[dealing_ref[b]],
             x_ref.at[b],
             routes_ref.at[b],
             *wholes[:5],
@@ -1019,15 +1042,48 @@
             gates_ref.at[b],
             table_ref,
         )
-        share(b, 2, token_refs.at[b], token_boxes.at[b])
-        share(b, 3, gates_ref.at[b], gate_boxes.at[b])
+        for part in keep(b):
+            part.start()
+
+        @pl.when(b == 0)
+        def _():
+            for kind in (2, 3):
+                share(0, kind).start()
+            for chunk in range(CHUNKS):
+                move_z(1, chunk)
+            dispatch(0, 0)
+
+        @pl.when(b == 1)
+        def _():
+            for kind in (2, 3):
+                share(1, kind).start()
+
+        return carry
+
+    def steps_of(b):
+        bit = PEER_BITS[DENSE_AXES[b]]
+        return [step for step in (7, 5, 6, 3, 4, 1, 2, 0) if not step & bit]
+
+    def row_copy(b, relayed, turn):
+        _, source = peer_of(PEER_BITS[DENSE_AXES[b]] if relayed else 0)
+        step = steps_of(b)[turn]
+        place = sent_refs.at[b, 4 * relayed + turn]
+        if step:
+            return send_later(
+                place,
+                arrived_ref.at[b, source],
+                row_send.at[b, 4 * relayed + turn],
+                row_recv.at[b, source],
+                peer_of(step)[0],
+            )
+        return pltpu.make_async_copy(
+            place, arrived_ref.at[b, source], local_sem.at[2 + 2 * b + relayed]
+        )
 
     def dispatch(b, relayed):
-        axis = DENSE_AXES[b]
-        bit = PEER_BITS[axis]
         if relayed:
             for kind in range(4):
-                shared[b, kind].wait_recv()
+                share(b, kind).wait_recv()
             fill = dispatcher(
                 experts,
                 capacity,
@@ -1045,33 +1101,11 @@
                 gates_ref.at[b],
                 routes_t_ref.at[b],
             )
-        _, source = peer_of(bit if relayed else 0)
-        steps = [step for step in (7, 5, 6, 3, 4, 1, 2, 0) if not step & bit]
-        for turn, step in enumerate(steps):
-            target, block = peer_of(step)
-            place = sent_refs.at[b, 4 * relayed + turn]
-            fill(block, place)
-            if step:
-                copy = send(
-                    place,
-                    arrived_ref.at[b, source],
-                    row_send.at[b, 4 * relayed + turn],
-                    row_recv.at[b, source],
-                    target,
-                )
-                flying.append(copy)
-            else:
-                copy = pltpu.make_async_copy(
-                    place, arrived_ref.at[b, source], local_sem.at[2 + 2 * b + relayed]
-                )
-                copy.start()
-                flying.append(copy)
-
-    forward(0)
-    for chunk in range(CHUNKS):
-        move_z(1, chunk)
-    dispatch(0, 0)
-    forward(1)
+        for turn, step in enumerate(steps_of(b)):
+            fill(peer_of(step)[1], sent_refs.at[b, 4 * relayed + turn])
+            row_copy(b, relayed, turn).start()
+
+    lax.fori_loop(0, batch, forward, 0)
     for chunk in range(CHUNKS):
         relay_z(0, chunk)
     dispatch(0, 1)
@@ -1094,16 +1128,19 @@
         for which in range(2):
             pltpu.make_async_copy(sources[which], outs[which][0], local_sem.at[which]).wait()
 
+    for part in (*keeps, *keep(0), *keep(1)):
+        part.wait()
     for copy in mixers:
         copy.wait_send()
-    for copy in flying:
-        if copy.is_remote:
-            copy.wait_send()
-        else:
-            copy.wait()
     for b in range(batch):
+        for relayed in range(2):
+            for turn, step in enumerate(steps_of(b)):
+                if step:
+                    row_copy(b, relayed, turn).wait_send()
+                else:
+                    row_copy(b, relayed, turn).wait()
         for kind in range(4):
-            shared[b, kind].wait_send()
+            share(b, kind).wait_send()
         bit = PEER_BITS[DENSE_AXES[b]]
         for step in range(8):
             if step & ~bit:
@@ -1141,8 +1178,8 @@
             shape((2, width), jnp.float32),
             shape(bias_shape, jnp.float32),
         ),
-        in_specs=[SMEM, *([VMEM] * (6 + count))],
-        out_specs=[*([VMEM] * count), *([anywhere] * 9), *([VMEM] * 9)],
+        in_specs=[SMEM, SMEM, *([VMEM] * (6 + count))],
+        out_specs=[*([anywhere] * 5), VMEM, *([anywhere] * 9), *([anywhere] * 6), *([VMEM] * 3)],
         scratch_shapes=[
             pltpu.VMEM((batch, *exchange), jnp.bfloat16),
             *([pltpu.VMEM(x.shape, jnp.bfloat16)] * 3),
@@ -1160,25 +1197,37 @@
             dma((6,)),
             dma((batch, 4)),
             dma((batch, 4)),
+            dma((5 + 6 * batch,)),
+            *([pltpu.VMEM(x.shape, jnp.bfloat16)] * 5),
+            pltpu.VMEM(x.shape, jnp.float32),
+            *(pltpu.VMEM(whole.shape, jnp.bfloat16) for whole in wholes[:5]),
         ],
         compiler_params=pltpu.CompilerParams(
             collective_id=1, has_side_effects=True, vmem_limit_bytes=60 * 2**20
         ),
         name="layer_head",
-    )(lengths, x, g, routes, routes_t, inner, outer, *parts)
+    )(*lengths, x, g, routes, routes_t, inner, outer, *parts)
     wholes, rest = results[:count], results[count:]
     return wholes, rest[:4], rest[4:8], rest[8], rest[9:16], rest[16], rest[17]
 
 
 def middle_kernel(arrived_ref, *refs):
-    inner_refs, outer_refs, refs = refs[:4], refs[4:8], refs[8:]
+    sources, refs = refs[:8], refs[8:]
     returned_ref, outs, refs = refs[0], refs[1:5], refs[5:]
     taken, going, inner_sums, outer_sums, refs = refs[0], refs[1], refs[2:6], refs[6:10], refs[10:]
-    stage, inbox, take_sem, send_sem, recv_sem, local_sem, core_send, core_recv = refs
+    stage, inbox, take_sem, send_sem, recv_sem, local_sem, core_send, core_recv = refs[:8]
+    fetch_sem, *weights = refs[8:]
+    inner_refs, outer_refs = weights[:4], weights[4:]
+    fetches = [
+        pltpu.make_async_copy(source, target, fetch_sem.at[index])
+        for index, (source, target) in enumerate(zip(sources, weights))
+    ]
+    for part in fetches:
+        part.start()
     y, zl, x = (lax.axis_index(axis) for axis in PEER_AXES)
     mine = y * 4 + zl * 2 + x
-    batch, sources, _, slots, width = arrived_ref.shape
-    groups = sources // 2
+    batch, blocks, _, slots, width = arrived_ref.shape
+    groups = blocks // 2
     total = batch * groups
 
     meet([across("core"), *(peer_of(step)[0] for step in range(1, 8))])
@@ -1246,6 +1295,8 @@
 
     for side in range(2):
         take(0, side).start()
+    for part in fetches:
+        part.wait()
 
     def work(i, carry):
         slot = lax.rem(i, 2)
@@ -1329,7 +1380,7 @@
             jax.ShapeDtypeStruct(arrived.shape, jnp.bfloat16),
             *([jax.ShapeDtypeStruct(quarter, jnp.bfloat16)] * 4),
         ),
-        in_specs=[anywhere, *([VMEM] * 8)],
+        in_specs=[anywhere] * 9,
         out_specs=[anywhere, *([VMEM] * 4)],
         scratch_shapes=[
             pltpu.VMEM((2, 2, 2, slots, width), jnp.bfloat16),
@@ -1343,6 +1394,8 @@
             dma((batch,)),
             dma((4,)),
             dma((4,)),
+            dma((8,)),
+            *([pltpu.VMEM(quarter, jnp.bfloat16)] * 8),
         ],
         compiler_params=pltpu.CompilerParams(
             collective_id=3, has_side_effects=True, vmem_limit_bytes=63 * 2**20
@@ -1373,7 +1426,7 @@
 FOLD_SPLIT = 4
 
 
-def tail_kernel(experts, capacity, bucket_count, lengths_ref, *refs):
+def tail_kernel(experts, capacity, bucket_count, lengths_ref, dealing_ref, *refs):
     x_ref, g_ref, routes_ref, refs = refs[0], refs[1], refs[2], refs[3:]
     weights, gain_ref, bias_ref, refs = refs[:5], refs[5], refs[6], refs[7:]
     normed_ref, q_ref, k_ref, v_ref, mix_ref, residual_ref, gates_ref, returned_ref = refs[:8]
@@ -1389,7 +1442,11 @@
     grad_mix, grad_residual, scratch, refs = refs[0], refs[1], refs[2:6], refs[6:]
     grads, sums, refs = refs[:8], refs[8:16], refs[16:]
     inboxes, refs = [refs[8 * i : 8 * i + 8] for i in range(5)], refs[40:]
-    fetched, landed, fold_send, fold_recv, move_send, move_recv, local_sem, own_sem = refs
+    fetched, landed, fold_send, fold_recv, move_send, move_recv, local_sem, own_sem = refs[:8]
+    fetch_sem, *fetch_to = refs[8:]
+    fetch_from = [mix_ref, q_ref, k_ref, v_ref, normed_ref, *weights[:3]]
+    mix_ref, q_ref, k_ref, v_ref, normed_ref = fetch_to[:5]
+    weights = [*fetch_to[5:], *weights[3:]]
     y, zh = lax.axis_index("y"), lax.axis_index("zh")
     at_home, away = zh == y, zh != y
     batch, tokens, width = x_ref.shape
@@ -1397,7 +1454,10 @@
     rows = far[0].shape[0] // CHUNKS
     cut_at = FOLD_SPLIT * LANES
 
-    greet(("core", "y", "x", "zl", "zh"))
+    fetches = [
+        pltpu.make_async_copy(source, target, fetch_sem.at[index])
+        for index, (source, target) in enumerate(zip(fetch_from, fetch_to))
+    ]
 
     def load(b):
         return [
@@ -1407,6 +1467,10 @@
 
     def piece(ref, chunk):
         return ref.at[pl.ds(chunk * rows, rows)]
+
+    for part in (*load(0), *fetches):
+        part.start()
+    greet(("core", "y", "x", "zl", "zh"))
 
     def own(which, chunk):
         return pltpu.make_async_copy(
@@ -1440,8 +1504,6 @@
     order = [(which, chunk) for which in range(2) for chunk in range(CHUNKS)]
     for which, chunk in order:
         copy(which, chunk, 0, far[which], fetched.at[which], "y").start()
-    for part in load(0):
-        part.start()
 
     def columns(ref, b, first):
         return ref.at[b, :, :cut_at] if first else ref.at[b, :, cut_at:]
@@ -1461,7 +1523,11 @@
     fold, fold_end = folder(operands, outs, grads, sums, inboxes, fold_send, fold_recv)
     early, late, small = (1, 2, 3), (4, 5, 6), 7
 
-    for b in range(batch):
+    def each(b, actions):
+        for index, action in enumerate(actions):
+            pl.when(b == index)(action)
+
+    def combine(b, carry):
         for part in load(b):
             part.wait()
         combine_math(
@@ -1482,24 +1548,34 @@
             gain_grad.at[b],
             grad_mix.at[b],
             grad_residual.at[b],
-        )
-        if b + 1 < batch:
-            for part in load(b + 1):
+            lambda: each(b, [lambda: move(0), lambda: move(2)]),
+        )
+
+        def first():
+            for part in load(1):
                 part.start()
-            move(0)
-        else:
+            move(1)
+
+        def second():
             for which, chunk in order:
                 own(which, chunk).start()
-            move(1)
+            move(3)
+
+        each(b, [first, second])
+        return carry
+
+    lax.fori_loop(0, batch, combine, 0)
+    for part in fetches:
+        part.wait()
     fold(0, 0)
 
     actions = {
-        0: [(fold, 0, 1), (move, 2)],
-        3: [(fold, 0, 2), (move, 3)],
-        5: [(move, 4)],
-        7: [*((fold, i, 0) for i in early), (move, 5)],
-        9: [*((fold, i, 1) for i in early), (fold, 0, 3)],
-        10: [(move, 6)],
+        0: [(fold, 0, 1), (move, 4)],
+        3: [(fold, 0, 2), (move, 5)],
+        6: [(move, 6)],
+        7: [*((fold, i, 0) for i in early)],
+        8: [(fold, 0, 3)],
+        9: [*((fold, i, 1) for i in early)],
         11: [*((fold, i, 2) for i in early), (move, 7)],
     }
 
@@ -1511,7 +1587,7 @@
         pair, b = item // 2, lax.rem(item, 2)
         attend_back_math(
             pair,
-            lengths_ref[b],
+            lengths_ref[dealing_ref[b]],
             q_ref.at[b],
             k_ref.at[b],
             v_ref.at[b],
@@ -1533,7 +1609,7 @@
     for i in early:
         fold(i, 3)
 
-    def finish(b):
+    def finish(b, carry):
         finish_math(
             x_ref.at[b],
             *weights[:3],
@@ -1546,11 +1622,14 @@
             input_grad_ref.at[b],
         )
 
-    finish(0)
-    for i in late:
-        fold(i, 1)
-    fold(0, 4)
-    finish(1)
+        @pl.when(b == 0)
+        def _():
+            for i in late:
+                fold(i, 1)
+
+        return carry
+
+    lax.fori_loop(0, batch, finish, 0)
     lines = [
         jnp.concatenate(
             [
@@ -1574,11 +1653,11 @@
     packed = jnp.concatenate([router_grad[0] + router_grad[1], stacked.T], 1)
     grads[small][...] = packed.astype(jnp.bfloat16).reshape(grads[small].shape)
     fold(small, 0)
-    reached = {0: 5, small: 1, **dict.fromkeys(early, 4), **dict.fromkeys(late, 2)}
-    while min(reached.values()) < FOLD_STEPS:
-        for i in (*late, small, *early, 0):
-            if reached[i] < FOLD_STEPS:
-                fold(i, reached[i])
+    reached = {0: 4, **dict.fromkeys(early, 4), **dict.fromkeys(late, 2), small: 1}
+    for k in range(1, FOLD_STEPS):
+        for i in reached:
+            if reached[i] == k:
+                fold(i, k)
                 reached[i] += 1
     fold_end()
 
@@ -1625,7 +1704,16 @@
             *([shape(quarter, jnp.bfloat16)] * 2),
             *(shape((2, 2, *size), jnp.bfloat16) for size in sizes),
         ),
-        in_specs=[SMEM, *([VMEM] * (3 + 5 + 2 + 7)), *([anywhere] * 5)],
+        in_specs=[
+            SMEM,
+            SMEM,
+            *([VMEM] * 3),
+            *([anywhere] * 3),
+            *([VMEM] * 4),
+            *([anywhere] * 5),
+            *([VMEM] * 2),
+            *([anywhere] * 5),
+        ],
         out_specs=[VMEM] * 12,
         scratch_shapes=[
             pltpu.VMEM(side, jnp.bfloat16),
@@ -1651,12 +1739,15 @@
             dma((2, CHUNKS, 2)),
             dma((2,)),
             dma((2, CHUNKS)),
+            dma((8,)),
+            *([pltpu.VMEM(x.shape, jnp.bfloat16)] * 5),
+            *([pltpu.VMEM(weights[0].shape, jnp.bfloat16)] * 3),
         ],
         compiler_params=pltpu.CompilerParams(
             collective_id=2, has_side_effects=True, vmem_limit_bytes=63 * 2**20
         ),
         name="layer_tail",
-    )(lengths, x, g, routes, *weights, gains, bias, *saved, returned, *partials)
+    )(*lengths, x, g, routes, *weights, gains, bias, *saved, returned, *partials)
     output, *rest, packed = (
         out.reshape(-1, out.shape[-1]).astype(jnp.float32) for out in results[4:]
     )
@@ -1670,6 +1761,7 @@
     swap_axes = "expert"
 
     def begin(self, sizes, lengths, x, g, routes, routes_t, inner, outer, parts, bias_shape):
+        lengths = jnp.take(*lengths)
         wholes = [lax.all_gather(part, "shard", axis=0, tiled=True) for part in parts]
         misc = wholes[5].reshape(-1, *parts[5].shape).astype(jnp.float32)
         gains = jnp.sum(misc[:, -2:], 0)
@@ -1719,6 +1811,7 @@
         outer,
         likes,
     ):
+        lengths = jnp.take(*lengths)
         returned, units = [], []
         for rows in arrived:
             going, *unit_pair = expert_pass(rows, inner, outer)
@@ -1874,12 +1967,10 @@
     ]
     heads = shards * position_bias.shape[0]
     bias_shape = (heads // 2, 2, seq_len // LANES, 2 * LANES)
-    seq_numbers = jnp.arange(lengths.shape[0], dtype=jnp.int32)
-    seq_lengths = jnp.sum(jnp.where(seq_numbers == dealing[:, None], lengths, 0), 1)
     sizes = (experts, capacity)
     wholes, inner_parts, outer_parts, arrived, saved, gains, bias_rows = plan.begin(
         sizes,
-        seq_lengths,
+        (lengths, dealing),
         tokens,
         cotangent,
         routes,
@@ -1892,7 +1983,7 @@
     results, input_grads, large_and_small, homes = plan.finish(
         sizes,
         bucket_count,
-        seq_lengths,
+        (lengths, dealing),
         tokens,
         cotangent,
         routes,

time: 480 us -> 467 us (0.973)
  Pallas kernels: 452 us -> 441 us
where the time goes in v2:
time: 467 us; the launch traced here: 462 us
  Pallas kernels  441 us (94%)
  local copies, waits for them, and re-layouts  11.4 us (2%)
  other arithmetic  7 us (1%)
    pallas_call x1, Pallas kernels, layer_head(): pl.pallas_call(functools.partial(head_kernel, experts, capacity), out_sha...  162 us
    pallas_call x1, Pallas kernels, layer_tail(): pl.pallas_call(functools.partial(tail_kernel, experts, capacity, bucket_c...  150 us
    pallas_call x1, Pallas kernels, layer_middle(): pl.pallas_call(middle_kernel, out_shape=(jax.ShapeDtypeStruct(arrived.sha...  129 us

profile of v2, /device:TPU:0, one launch (start us, length us, event | category | flops | bytes accessed | tf_op | source)
XLA Modules:
  0.0 461.9 jit_solution(966156792741165140)
XLA Ops:
  0.6 0.0 copy-start
  0.7 0.7 stack.9
  1.3 0.7 stack.10
  2.0 0.1 tile.10
  2.1 0.0 copy-done
  2.1 1.0 fusion
  3.2 1.3 pad.12.routes_t_ref
  4.5 0.6 fusion.3.refs_5_
  5.1 0.8 copy.33
  5.9 0.6 pad.13.refs_4_
  6.6 1.6 copy.35.routes_ref.refs_2_
  8.2 162.3 %layer_head.1 = (bf16[768,768]{1,0:T(8,128)(2,1)}, bf16[768,768]{1,0:T(8,128)(2,1)}, bf16[768,768]{1,0:T(8,128)(2,1)}, bf16[768,768]{1,0:T(8,128)(2,1)}, bf16[76...) custom-call(s32[64]{0:T(128)} %lengths_ref.3, ...), custom_call_target="tpu_custom_call" | custom-call | tf_op jit(solution)/shard_map/layer_head/pallas_call | solution.py:1169
  170.5 129.1 %layer_middle.1 = (bf16[2,8,2,192,768]{4,3,2,1,0:T(8,128)(2,1)}, bf16[768,768]{1,0:T(8,128)(2,1)}, bf16[768,768]{1,0:T(8,128)(2,1)}, bf16[768,768]{1,0:T(8,128)(2,1)}, bf16[768,768]{1,0:T(8,128)(2,1)}) custom-call(bf16[2,8,2,192,768]{4,3,2,1,0:T(8,128)(2,1)} %get-tuple-element.66.arrived_ref, bf16[768,768]{1,0:T(8,128)(2,1)} %get-tuple-element.67.refs_0_, ...), custom_call_target="tpu_custom_call" | custom-call | tf_op jit(solution)/shard_map/layer_middle/pallas_call | solution.py:1377
  299.6 150.0 %layer_tail.1 = (bf16[2,384,768]{2,1,0:T(8,128)(2,1)}, bf16[2,384,768]{2,1,0:T(8,128)(2,1)}, bf16[768,768]{1,0:T(8,128)(2,1)}, bf16[768,768]{1,0:T(8,128)(2,1)},...) custom-call(s32[64]{0:T(128)} %lengths_ref.3, ...), custom_call_target="tpu_custom_call" | custom-call | tf_op jit(solution)/shard_map/layer_tail/pallas_call | solution.py:1699
  449.7 0.0 copy-start.9
  449.7 0.0 copy-start.12
  449.7 1.0 bitcast_convert_fusion.3
  450.7 0.2 slice_reduce_fusion
  450.8 0.7 reshape_squeeze.3
  451.5 0.7 copy.40
  452.2 0.1 fusion.8
  452.3 0.6 copy.42
  452.9 0.6 copy.41
  453.6 0.0 copy-done.9
  453.6 0.9 maximum_convert_fusion.2
  454.4 0.9 bitcast_convert_fusion.2
  455.3 0.0 copy-done.10
  455.3 1.1 maximum_convert_fusion
  456.4 2.5 bitcast_convert_fusion
  459.0 1.0 copy.47
  460.0 0.7 copy-done.4
  460.7 1.0 copy.48
  (24 shorter events, 0.1 us)
Async XLA Ops:
  0.6 1.5 copy-start
  449.7 3.9 copy-start.9
  449.7 3.9 copy-start.12
  449.7 4.8 %copy-start.6 = (bf16[2,2,48,768]{3,2,1,0:T(8,128)(2,1)S(1)}, bf16[2,2,48,768]{3,2,1,0:T(8,128)(2,1)}, u32[]{:S(2)}) copy-start(bf16[2,2,48,768]{3,2,1,0:T(8,128)(2,1)} %get-tuple-element.88) | copy-start | bytes 884740
  452.2 3.1 copy-start.7
  452.2 3.1 copy-start.8
  452.2 3.1 copy-start.10
  452.2 3.1 copy-start.11
  454.4 2.0 copy-start.2
  454.4 2.0 copy-start.3
  456.4 2.5 copy-start.5
  459.0 1.7 copy-start.4
  459.0 2.7 copy-start.1

commit v3 on v2

--- a/solution.py
+++ b/solution.py
@@ -869,7 +869,7 @@
     sent_refs, token_refs, token_boxes, g_boxes, gate_boxes, route_boxes = refs[:6]
     relays, table_ref, refs = refs[6:8], refs[8], refs[9:]
     mixer_send, mixer_recv, move_send, move_recv, row_send, row_recv, local_sem = refs[:7]
-    share_send, share_recv, keep_sem, *kept = refs[7:]
+    share_send, share_recv, keep_sem, gate_lines, *kept = refs[7:]
     normed_ref, q_ref, k_ref, v_ref, mix_ref, residual_ref = kept[:6]
     whole_targets, wholes = wholes[:5], [*kept[6:], wholes[5]]
     core, y, x, zh = (lax.axis_index(axis) for axis in ("core", "y", "x", "zh"))
@@ -954,7 +954,7 @@
         return whole.at[pl.ds(pl.multiple_of(start, size), size)]
 
     def share(b, kind):
-        source = (g_ref, routes_t_ref, token_refs, gates_ref)[kind]
+        source = (g_ref, routes_t_ref, token_refs, gate_lines)[kind]
         box = (g_boxes, route_boxes, token_boxes, gate_boxes)[kind]
         return send_later(
             source.at[b],
@@ -1042,6 +1042,7 @@
             gates_ref.at[b],
             table_ref,
         )
+        gate_lines[b] = gates_ref[b].T[: gate_lines.shape[1]]
         for part in keep(b):
             part.start()
 
@@ -1089,7 +1090,7 @@
                 capacity,
                 token_boxes.at[b],
                 g_boxes.at[b],
-                gate_boxes.at[b],
+                jnp.concatenate([gate_boxes[b], jnp.zeros((LANES - 8, tokens), jnp.float32)], 0).T,
                 route_boxes.at[b],
             )
         else:
@@ -1183,7 +1184,7 @@
         scratch_shapes=[
             pltpu.VMEM((batch, *exchange), jnp.bfloat16),
             *([pltpu.VMEM(x.shape, jnp.bfloat16)] * 3),
-            pltpu.VMEM((batch, tokens, LANES), jnp.float32),
+            pltpu.VMEM((batch, 8, tokens), jnp.float32),
             pltpu.VMEM(routes_t.shape, jnp.int32),
             pltpu.VMEM(inner.shape, jnp.bfloat16),
             pltpu.VMEM(outer.shape, jnp.bfloat16),
@@ -1198,6 +1199,7 @@
             dma((batch, 4)),
             dma((batch, 4)),
             dma((5 + 6 * batch,)),
+            pltpu.VMEM((batch, 8, tokens), jnp.float32),
             *([pltpu.VMEM(x.shape, jnp.bfloat16)] * 5),
             pltpu.VMEM(x.shape, jnp.float32),
             *(pltpu.VMEM(whole.shape, jnp.bfloat16) for whole in wholes[:5]),

time: 467 us -> 464 us (level)
  no operation moved by 1% of the time
where the time goes in v3:
time: 464 us; the launch traced here: 458 us
  Pallas kernels  438 us (94%)
  local copies, waits for them, and re-layouts  11.4 us (2%)
  other arithmetic  7 us (2%)
    pallas_call x1, Pallas kernels, layer_head(): pl.pallas_call(functools.partial(head_kernel, experts, capacity), out_sha...  158 us
    pallas_call x1, Pallas kernels, layer_tail(): pl.pallas_call(functools.partial(tail_kernel, experts, capacity, bucket_c...  150 us
    pallas_call x1, Pallas kernels, layer_middle(): pl.pallas_call(middle_kernel, out_shape=(jax.ShapeDtypeStruct(arrived.sha...  129 us

profile of v3, /device:TPU:0, one launch (start us, length us, event | category | flops | bytes accessed | tf_op | source)
XLA Modules:
  0.0 458.0 jit_solution(1444915338760383600)
XLA Ops:
  0.6 0.0 copy-start
  0.7 0.7 stack.9
  1.3 0.7 stack.10
  2.0 0.1 tile.10
  2.1 1.0 fusion
  3.2 1.3 pad.12.routes_t_ref
  4.5 0.6 fusion.3.refs_5_
  5.1 0.8 copy.33
  5.9 0.6 pad.13.refs_4_
  6.6 1.6 copy.35.routes_ref.refs_2_
  8.2 158.4 %layer_head.1 = (bf16[768,768]{1,0:T(8,128)(2,1)}, bf16[768,768]{1,0:T(8,128)(2,1)}, bf16[768,768]{1,0:T(8,128)(2,1)}, bf16[768,768]{1,0:T(8,128)(2,1)}, bf16[76...) custom-call(s32[64]{0:T(128)} %lengths_ref.3, ...), custom_call_target="tpu_custom_call" | custom-call | tf_op jit(solution)/shard_map/layer_head/pallas_call | solution.py:1170
  166.6 129.1 %layer_middle.1 = (bf16[2,8,2,192,768]{4,3,2,1,0:T(8,128)(2,1)}, bf16[768,768]{1,0:T(8,128)(2,1)}, bf16[768,768]{1,0:T(8,128)(2,1)}, bf16[768,768]{1,0:T(8,128)(2,1)}, bf16[768,768]{1,0:T(8,128)(2,1)}) custom-call(bf16[2,8,2,192,768]{4,3,2,1,0:T(8,128)(2,1)} %get-tuple-element.66.arrived_ref, bf16[768,768]{1,0:T(8,128)(2,1)} %get-tuple-element.67.refs_0_, ...), custom_call_target="tpu_custom_call" | custom-call | tf_op jit(solution)/shard_map/layer_middle/pallas_call | solution.py:1379
  295.7 150.1 %layer_tail.1 = (bf16[2,384,768]{2,1,0:T(8,128)(2,1)}, bf16[2,384,768]{2,1,0:T(8,128)(2,1)}, bf16[768,768]{1,0:T(8,128)(2,1)}, bf16[768,768]{1,0:T(8,128)(2,1)},...) custom-call(s32[64]{0:T(128)} %lengths_ref.3, ...), custom_call_target="tpu_custom_call" | custom-call | tf_op jit(solution)/shard_map/layer_tail/pallas_call | solution.py:1701
  445.8 1.0 bitcast_convert_fusion.3
  446.8 0.2 slice_reduce_fusion
  447.0 0.7 reshape_squeeze.3
  447.6 0.7 copy.40
  448.3 0.1 fusion.8
  448.4 0.6 copy.42
  449.1 0.6 copy.41
  449.7 0.9 maximum_convert_fusion.2
  450.6 0.0 copy-done.6
  450.6 0.9 bitcast_convert_fusion.2
  451.4 0.0 copy-done.8
  451.4 0.0 copy-done.11
  451.5 1.1 maximum_convert_fusion
  452.5 0.0 copy-done.3
  452.6 2.5 bitcast_convert_fusion
  455.1 1.0 copy.47
  456.1 0.7 copy-done.4
  456.8 1.0 copy.48
  457.8 0.0 copy-done.1
  (24 shorter events, 0.1 us)
Async XLA Ops:
  0.6 1.5 copy-start
  445.8 3.9 copy-start.9
  445.8 3.9 copy-start.12
  445.8 4.8 %copy-start.6 = (bf16[2,2,48,768]{3,2,1,0:T(8,128)(2,1)S(1)}, bf16[2,2,48,768]{3,2,1,0:T(8,128)(2,1)}, u32[]{:S(2)}) copy-start(bf16[2,2,48,768]{3,2,1,0:T(8,128)(2,1)} %get-tuple-element.88) | copy-start | bytes 884740
  448.3 3.1 copy-start.7
  448.3 3.1 copy-start.8
  448.3 3.1 copy-start.10
  448.3 3.1 copy-start.11
  450.6 2.0 copy-start.2
  450.6 2.0 copy-start.3
  452.5 2.5 copy-start.5
  455.1 1.7 copy-start.4
  455.1 2.7 copy-start.1
